TPU v7x, 256 devices: a whole 4x4x8 slice. The times are simulated.
256 devices in a mesh: tower: 2 (over x_lo), blk: 128 (over z, y, x_hi, core).
Axes of the slice: x: 4 (x_hi: 2, x_lo: 2; x = x_hi * 2 + x_lo), y: 4, z: 8, core: 2. Of those that a mesh axis runs over, the one named last changes fastest.
Arguments:
- pooled: bfloat16 [2, 16384, 1152], P('tower', 'blk'), may hold values from -6 to 6
- final_gain: float32 [2, 1152], P('tower'), may hold values from 0.5 to 1.5
- head_weight: bfloat16 [2, 1152, 1152], P('tower'), may hold values from -0.1875 to 0.1875
- pair_ids: int32 [16384], replicated, may hold values from 0 to 16383
- log_scale: float32 [1], replicated, may hold values from 4.2 to 4.7
- bias: float32 [1], replicated, may hold values from -4 to -1
Outputs:
- emb_grad: float32 [2, 16384, 1152], P('tower', 'blk')
Inputs may be any that keep to these rules, and one draw needn't show every extreme that they name: `pair_ids`: examples with equal ids form positive pairs; every example is a positive pair with its own image and text.
All inputs are finite; a program needn't handle non-finite values.
Results may differ from a plain program's by a relative error of at most 0.0043.
Values may be sent and summed in bfloat16 or wider, within the bound.
No kernel may reach another device: no remote copies, remote signals or barrier semaphores. Data moves between devices by JAX's collectives and lax.ppermute only.
A program may use at most 192 MiB of HBM per device.

v0:
```python
import jax
import jax.numpy as jnp
from jax import lax
from jax.sharding import PartitionSpec as P


NZ, NY, NH, NC = 8, 4, 2, 2
BLK = NZ * NY * NH * NC


def hop(value, route):
    pairs = []
    for m in range(2):
        for b in range(BLK):
            c, h, y, z = b % NC, b // NC % NH, b // (NC * NH) % NY, b // (NC * NH * NY)
            goal = route(m, z, y, h, c)
            if goal is None:
                continue
            tm, tz, ty, th, tc = goal
            target = ((tz % NZ * NY + ty % NY) * NH + th) * NC + tc
            pairs.append((m * BLK + b, tm * BLK + target))
    return lax.ppermute(value, ("tower", "blk"), pairs)


def embed_rows(feats, gain, weight):
    values = feats.astype(jnp.float32)
    center = values - jnp.mean(values, axis=-1, keepdims=True)
    spread = jnp.mean(center * center, axis=-1, keepdims=True)
    normed = (center * lax.rsqrt(spread + 1e-06) * gain).astype(jnp.bfloat16)
    head = jnp.dot(normed, weight, preferred_element_type=jnp.float32)
    length = jnp.sum(head * head, axis=-1, keepdims=True)
    return (head * lax.rsqrt(length + 1e-06)).astype(jnp.bfloat16)


def pair_coef(image_rows, text_rows, image_ids, text_ids, scale, shift):
    logits = (
        scale
        * lax.dot_general(
            image_rows, text_rows, (((1,), (1,)), ((), ())), preferred_element_type=jnp.float32
        )
        + shift
    )
    match = image_ids[:, None] == text_ids[None, :]
    share = jax.nn.sigmoid(jnp.where(match, -logits, logits))
    return jnp.where(match, -share, share).astype(jnp.bfloat16)


def up_y(m, z, y, h, c):
    return (m, z, y + 1, h, c)


def down_y(m, z, y, h, c):
    return (m, z, y - 1, h, c)


def two_y(m, z, y, h, c):
    return (m, z, y + 2, h, c)


def ring_z(m, z, y, h, c):
    return (m, z - 1 if c else z + 1, y, h, c)


def unring_z(m, z, y, h, c):
    return (m, z + 1 if c else z - 1, y, h, c)


def ring2_z(m, z, y, h, c):
    return (m, z - 2 if c else z + 2, y, h, c)


def unring2_z(m, z, y, h, c):
    return (m, z + 2 if c else z - 2, y, h, c)


def swap(m, z, y, h, c):
    return (m, z, y, h, 1 - c)


def to_spread(m, z, y, h, c):
    if not m:
        return (1, z, y, h, 1) if c else None
    return (0, z, y, h if c else 1 - h, c)


def from_spread(m, z, y, h, c):
    if m:
        return (0, z, y, h, 1) if c else None
    return (1, z, y, h if c else 1 - h, c)


def forward(m, z, y, h, c):
    return None if m else (1, z, y, 1 - h if c else h, c)


def to_same(m, z, y, h, c):
    return (1, z, y, 1 - h, c) if m else None


def to_column(m, z, y, h, c):
    return (0, z, y, 1 - h if c else h, c) if m else None


def from_column(m, z, y, h, c):
    return None if m else (1, z, y, 1 - h if c else h, c)


def spread_y(block):
    below = hop(block, up_y)
    above = hop(block, down_y)
    far = hop(block, two_y)
    return jnp.concatenate([block, below, above, far])


def collect_y(part, ex):
    send = part[ex:].astype(jnp.bfloat16)
    below = hop(send[:ex], down_y)
    above = hop(send[ex : 2 * ex], up_y)
    far = hop(send[2 * ex :], two_y)
    return part[:ex] + below.astype(jnp.float32) + above.astype(jnp.float32) + far.astype(jnp.float32)


def pick(table, order, size):
    wanted = order[:, None] == jnp.arange(size, dtype=jnp.int32)[None, :]
    return jnp.sum(jnp.where(wanted[:, :, None], table[None], 0), axis=1)


def tile(pooled, final_gain, head_weight, pair_ids, log_scale, bias):
    bf16, f32 = jnp.bfloat16, jnp.float32
    local = embed_rows(pooled[0], final_gain[0], head_weight[0])
    ex = local.shape[0]
    half = ex // 2
    scale = jnp.exp(log_scale[0])
    shift = bias[0]
    m = lax.axis_index("tower")
    b = lax.axis_index("blk")
    c, h, y, z = b & 1, (b >> 1) & 1, (b >> 2) & 3, b >> 4
    first = c == 0
    image_side = m == 0
    side = jnp.where(image_side & (c == 1), h, 1 - h)

    def mine(value):
        return jnp.where(first, value[:half], value[half:])

    def whole(own, other):
        return jnp.where(
            first, jnp.concatenate([own, other]), jnp.concatenate([other, own])
        )

    near = hop(local, to_spread)
    column = spread_y(local)
    kept = jnp.where(image_side, local, near)
    image = jnp.where(c == m, kept, hop(kept, swap))
    across = hop(near, forward)
    near, image = lax.optimization_barrier((near, image))
    r1 = hop(image, ring_z)
    r2 = hop(image, ring2_z)
    spread = spread_y(jnp.where(image_side, near, across))
    other = hop(column, to_column)
    r3 = hop(r2, ring_z)
    r4 = hop(mine(r2), ring2_z)
    s12 = hop(jnp.concatenate([r1, r2]), swap)
    got = hop(jnp.concatenate([r3, r4]), swap)
    image_rows = jnp.concatenate([image, r1, r2, s12, r3, got[:ex], whole(r4, got[ex:])])
    text_rows = jnp.concatenate([spread, jnp.where(image_side, other, column)])

    ids = pair_ids.reshape(NZ, NY, NH, NC, ex)
    image_col = lax.dynamic_slice(ids, (0, y, h, m, 0), (NZ, 1, 1, 1, ex)).reshape(NZ, ex)
    way = jnp.where(first, -1, 1)
    image_ids = pick(
        image_col, (z + way * jnp.array([0, 1, 2, -1, -2, 3, -3, 4], jnp.int32)) & 7, NZ
    ).reshape(NZ * ex)
    text_col = lax.dynamic_slice(ids, (z, 0, 0, c, 0), (1, NY, NH, 1, ex)).reshape(NY * NH, ex)
    text_ids = pick(
        text_col,
        ((y + jnp.array([0, -1, 1, 2, 0, -1, 1, 2], jnp.int32)) & 3) * 2
        + (side ^ jnp.array([0, 0, 0, 0, 1, 1, 1, 1], jnp.int32)),
        NY * NH,
    ).reshape(NY * NH * ex)

    coef = pair_coef(image_rows, text_rows, image_ids, text_ids, scale, shift)
    text_part = lax.dot_general(
        coef, image_rows, (((0,), (0,)), ((), ())), preferred_element_type=f32
    )
    image_part = jnp.dot(coef, text_rows, preferred_element_type=f32)

    part = [image_part[k * ex : (k + 1) * ex] for k in range(NZ)]
    theirs = jnp.where(first, part[7][half:], part[7][:half])
    got = hop(jnp.concatenate([part[3], part[4], part[6], theirs]).astype(bf16), swap)
    r3 = hop((part[5] + got[2 * ex : 3 * ex]).astype(bf16), unring_z)
    r4 = hop((mine(part[7]) + got[3 * ex :]).astype(bf16), unring2_z)
    r1 = hop((part[1] + got[:ex]).astype(bf16), unring_z)
    r2 = part[2] + got[ex : 2 * ex].astype(f32) + r3.astype(f32) + whole(r4, jnp.zeros_like(r4))
    r2 = hop(r2.astype(bf16), unring2_z)
    image_sum = part[0] + r1.astype(f32) + r2.astype(f32)

    column_part = text_part[NY * ex :]
    column_part = column_part + hop(column_part.astype(bf16), from_column)
    spread_sum = collect_y(text_part[: NY * ex], ex)
    text_sum = collect_y(column_part, ex)
    spread_sum = lax.optimization_barrier(spread_sum.astype(bf16))
    across = hop(spread_sum, to_same)
    image_sum = image_sum + hop(image_sum.astype(bf16), swap)
    near = hop(jnp.where(image_side, spread_sum, image_sum.astype(bf16)), from_spread)
    near = near.astype(f32)
    image_grad = jnp.where(first, image_sum, near)
    text_grad = text_sum + near + across.astype(f32)
    return jnp.where(image_side, image_grad, text_grad)[None]


def solution(mesh):
    placed = (P("tower", "blk", None), P("tower", None), P("tower", None, None), P(), P(), P())
    return jax.shard_map(
        tile, mesh=mesh, in_specs=placed, out_specs=P("tower", "blk", None), check_vma=False
    )
```

profile of v0, /device:TPU:107, one launch (start us, length us, event | category | flops | bytes accessed | tf_op | source)
XLA Modules:
  0.0 132.5 jit_solution(16002265841008508936)
XLA Ops:
  0.0 1.2 convert_reduce_fusion
  1.3 1.2 fusion.15
  2.5 0.7 reduce.1
  3.2 1.7 %multiply_reduce_fusion = (f32[128]{0:T(128)S(1)}, f32[128,1152]{1,0:T(8,128)S(1)}) fusion(bf16[1,1152,1152]{2,1,0:T(8,128)(2,1)S(1)} %copy-done, bf16[1,128,1152]{2,1,0:T(8,128)(2,1)} %param.9, f32[1152]{0:T(1024)S(1)} %reduce.1, f32[128]{0:T(128)S(1)} %add_rsqrt_fusion.1, f32[128]{0:T(128)S(1)} %broadcast_multiply_fusion), kind=kOutput, calls=%fused_computation.48 | convolution fusion | flops 340770688 | bytes 3545088 | tf_op jit(solution)/shard_map/dot_general | solution.py:30
  4.9 0.1 multiply_convert_fusion
  5.0 2.2 %collective-permute-start = (bf16[128,1152]{1,0:T(8,128)(2,1)S(1)}, bf16[128,1152]{1,0:T(8,128)(2,1)}, u32[]{:S(2)}, u32[]{:S(2)}) collective-permute-start(bf16[128,1152]{1,0:T(8,128)(2,1)S(1)} %multiply_convert_fusion), channel_id=1, source_target_pairs={{1,129},{3,131},{5,133},{7,135},{9,137},{11,139},{13,141},{15,143}... | collective-permute-start | bytes 884744 | tf_op jit(solution)/shard_map/ppermute | solution.py:22
  7.2 2.1 %collective-permute-start.14 = (bf16[128,1152]{1,0:T(8,128)(2,1)S(1)}, bf16[128,1152]{1,0:T(8,128)(2,1)}, u32[]{:S(2)}, u32[]{:S(2)}) collective-permute-start(bf16[128,1152]{1,0:T(8,128)(2,1)S(1)} %multiply_convert_fusion), channel_id=1, source_target_pairs={{0,8},{1,9},{2,10},{3,11},{4,12},{5,13},{6,14},{7,15},{8,0},{9,1},... | collective-permute-start | bytes 884744 | tf_op jit(solution)/shard_map/ppermute | solution.py:22
  9.3 1.1 collective-permute-start.13
  10.4 0.4 collective-permute-start.12
  10.9 0.7 constant_dynamic-slice_fusion
  11.7 0.7 constant_dynamic-slice_fusion.1
  12.5 0.1 collective-permute-done
  12.6 1.8 %broadcast_select_fusion.2 = bf16[128,1152]{1,0:T(8,128)(2,1)} fusion(bf16[128,1152]{1,0:T(8,128)(2,1)} %collective-permute-done, pred[]{:T(512)S(6)} %eq.63, f32[128,1152]{1,0:T(8,128)S(1)} %get-tuple-element.22, f32[128]{0:T(128)S(1)} %add_rsqrt_fusion), kind=kLoop, calls=%fused_computation.63 | loop fusion | flops 442368 | bytes 1180161 | tf_op jit(solution)/shard_map/jit(_where)/select_n | solution.py:152
  14.4 3.2 %collective-permute-start.1 = (bf16[128,1152]{1,0:T(8,128)(2,1)}, bf16[128,1152]{1,0:T(8,128)(2,1)S(1)}, u32[]{:S(2)}, u32[]{:S(2)}) collective-permute-start(bf16[128,1152]{1,0:T(8,128)(2,1)} %broadcast_select_fusion.2), channel_id=1, source_target_pairs={{0,1},{1,0},{2,3},{3,2},{4,5},{5,4},{6,7},{7,6},{8,9},{9,8},{10,11... | collective-permute-start | bytes 884744 | tf_op jit(solution)/shard_map/ppermute | solution.py:22
  19.1 4.9 %collective-permute-done.13 = bf16[128,1152]{1,0:T(8,128)(2,1)} collective-permute-done((bf16[128,1152]{1,0:T(8,128)(2,1)S(1)}, bf16[128,1152]{1,0:T(8,128)(2,1)}, u32[]{:S(2)}, u32[]{:S(2)}) %collective-permute-start.13) | collective-permute-done | bytes 294944 | tf_op jit(solution)/shard_map/ppermute | solution.py:22
  24.0 1.2 pad_maximum_fusion
  25.3 3.7 %collective-permute-start.15 = (bf16[512,1152]{1,0:T(8,128)(2,1)S(1)}, bf16[512,1152]{1,0:T(8,128)(2,1)S(1)}, u32[]{:S(2)}, u32[]{:S(2)}) collective-permute-start(bf16[512,1152]{1,0:T(8,128)(2,1)S(1)} %pad_maximum_fusion), channel_id=1, source_target_pairs={{128,0},{129,3},{130,2},{131,1},{132,4},{133,7},{134,6},{135,5},{1... | collective-permute-start | bytes 3538952 | tf_op jit(solution)/shard_map/ppermute | solution.py:22
  29.0 1.3 collective-permute-start.8
  30.3 1.0 broadcast_select_fusion
  31.5 5.5 %collective-permute-done.8 = bf16[128,1152]{1,0:T(8,128)(2,1)S(1)} collective-permute-done((bf16[128,1152]{1,0:T(8,128)(2,1)}, bf16[128,1152]{1,0:T(8,128)(2,1)S(1)}, u32[]{:S(2)}, u32[]{:S(2)}) %collective-permute-start.8) | collective-permute-done | bytes 294944 | tf_op jit(solution)/shard_map/ppermute | solution.py:22
  37.0 1.4 %collective-permute-start.9 = (bf16[128,1152]{1,0:T(8,128)(2,1)S(1)}, bf16[128,1152]{1,0:T(8,128)(2,1)S(1)}, u32[]{:S(2)}, u32[]{:S(2)}) collective-permute-start(bf16[128,1152]{1,0:T(8,128)(2,1)S(1)} %get-tuple-element.12), channel_id=1, source_target_pairs={{0,4},{1,5},{2,6},{3,7},{4,8},{5,9},{6,10},{7,11},{8,12},{9,13},{1... | collective-permute-start | bytes 884744 | tf_op jit(solution)/shard_map/ppermute | solution.py:22
  38.4 0.2 collective-permute-start.10
  38.6 2.1 %collective-permute-start.11 = (bf16[128,1152]{1,0:T(8,128)(2,1)S(1)}, bf16[128,1152]{1,0:T(8,128)(2,1)S(1)}, u32[]{:S(2)}, u32[]{:S(2)}) collective-permute-start(bf16[128,1152]{1,0:T(8,128)(2,1)S(1)} %get-tuple-element.12), channel_id=1, source_target_pairs={{0,8},{1,9},{2,10},{3,11},{4,12},{5,13},{6,14},{7,15},{8,0},{9,1},... | collective-permute-start | bytes 884744 | tf_op jit(solution)/shard_map/ppermute | solution.py:22
  40.7 2.5 %collective-permute-done.3 = bf16[128,1152]{1,0:T(8,128)(2,1)S(1)} collective-permute-done((bf16[128,1152]{1,0:T(8,128)(2,1)S(1)}, bf16[128,1152]{1,0:T(8,128)(2,1)S(1)}, u32[]{:S(2)}, u32[]{:S(2)}) %collective-permute-start.3) | collective-permute-done | bytes 294944 | tf_op jit(solution)/shard_map/ppermute | solution.py:22
  43.3 0.7 collective-permute-start.4
  44.0 1.1 collective-permute-done.9
  45.1 1.1 collective-permute-start.6
  46.3 0.4 collective-permute-start.5
  46.7 6.5 %collective-permute-done.11 = bf16[128,1152]{1,0:T(8,128)(2,1)S(1)} collective-permute-done((bf16[128,1152]{1,0:T(8,128)(2,1)S(1)}, bf16[128,1152]{1,0:T(8,128)(2,1)S(1)}, u32[]{:S(2)}, u32[]{:S(2)}) %collective-permute-start.11) | collective-permute-done | bytes 294944 | tf_op jit(solution)/shard_map/ppermute | solution.py:22
  53.2 2.6 %collective-permute-done.5 = bf16[128,1152]{1,0:T(8,128)(2,1)S(1)} collective-permute-done((bf16[128,1152]{1,0:T(8,128)(2,1)S(1)}, bf16[128,1152]{1,0:T(8,128)(2,1)S(1)}, u32[]{:S(2)}, u32[]{:S(2)}) %collective-permute-start.5) | collective-permute-done | bytes 294944 | tf_op jit(solution)/shard_map/ppermute | solution.py:22
  55.9 3.8 %collective-permute-start.7 = (bf16[192,1152]{1,0:T(8,128)(2,1)S(1)}, bf16[192,1152]{1,0:T(8,128)(2,1)S(1)}, u32[]{:S(2)}, u32[]{:S(2)}) collective-permute-start(bf16[192,1152]{1,0:T(8,128)(2,1)S(1)} %pad_maximum_fusion.3), channel_id=1, source_target_pairs={{0,1},{1,0},{2,3},{3,2},{4,5},{5,4},{6,7},{7,6},{8,9},{9,8},{10,11... | collective-permute-start | bytes 1327112 | tf_op jit(solution)/shard_map/ppermute | solution.py:22
  59.7 1.5 %select_dynamic-update-slice_fusion = bf16[1024,1152]{1,0:T(8,128)(2,1)S(1)} fusion(bf16[1024,1152]{1,0:T(8,128)(2,1)S(1)} %constant_dynamic-update-slice_fusion.5, bf16[512,1152]{1,0:T(8,128)(2,1)S(1)} %collective-permute-done.15, pred[]{:T(512)S(6)} %eq.63, bf16[128,1152]{1,0:T(8,128)(2,1)} %collective-permute-done.14, ...), kind=kLoop, calls=%fused_computation.12 | loop fusion | flops 5308416 | bytes 3538945 | tf_op jit(solution)/shard_map/concatenate | solution.py:165
  61.4 4.1 %fusion.4 = bf16[1024,1024]{1,0:T(8,128)(2,1)S(1)} fusion(bf16[1024,1152]{1,0:T(8,128)(2,1)S(1)} %fusion.31, bf16[1024,1152]{1,0:T(8,128)(2,1)S(1)} %select_dynamic-update-slice_fusion, f32[]{:T(128)} %bitcast.33, f32[]{:T(128)} %bitcast.5, s32[1024]{0:T(1024)S(1)} %bitcast.36, s32[1024]{0:T(1024)S(1)} %bitcast.37), kind=kOutput, calls=%fused_computation.6 | convolution fusion | flops 2427453440 | bytes 6823944 | tf_op jit(solution)/shard_map/dot_general | solution.py:38
  65.5 2.9 %fusion.40 = (bf16[1024,1152]{1,0:T(8,128)(2,1)S(1)}, f32[1024,1152]{1,0:T(8,128)S(1)}) fusion(bf16[1024,1024]{1,0:T(8,128)(2,1)S(1)} %fusion.4, bf16[1024,1152]{1,0:T(8,128)(2,1)S(1)} %select_dynamic-update-slice_fusion), kind=kOutput, calls=%fused_computation.90 | convolution fusion | flops 2417098752 | bytes 11534336 | tf_op jit(solution)/shard_map/dot_general | solution.py:185
  68.6 0.2 collective-permute-start.16
  68.8 3.0 %fusion.39 = (bf16[1024,1152]{1,0:T(8,128)(2,1)S(1)}, f32[1024,1152]{1,0:T(8,128)S(1)}) fusion(bf16[1024,1024]{1,0:T(8,128)(2,1)S(1)} %fusion.4, bf16[1024,1152]{1,0:T(8,128)(2,1)S(1)} %fusion.31), kind=kOutput, calls=%fused_computation.89 | convolution fusion | flops 2417098752 | bytes 11534336 | tf_op jit(solution)/shard_map/dot_general | solution.py:182
  71.9 4.3 %collective-permute-start.24 = (bf16[128,1152]{1,0:T(8,128)(2,1)S(1)}, bf16[128,1152]{1,0:T(8,128)(2,1)S(1)}, u32[]{:S(2)}, u32[]{:S(2)}) collective-permute-start(bf16[128,1152]{1,0:T(8,128)(2,1)S(1)} %get-tuple-element.16), channel_id=1, source_target_pairs={{0,8},{1,9},{2,10},{3,11},{4,12},{5,13},{6,14},{7,15},{8,0},{9,1},... | collective-permute-start | bytes 884744 | tf_op jit(solution)/shard_map/ppermute | solution.py:22
  76.2 2.6 %collective-permute-start.23 = (bf16[128,1152]{1,0:T(8,128)(2,1)S(1)}, bf16[128,1152]{1,0:T(8,128)(2,1)S(1)}, u32[]{:S(2)}, u32[]{:S(2)}) collective-permute-start(bf16[128,1152]{1,0:T(8,128)(2,1)S(1)} %get-tuple-element.17), channel_id=1, source_target_pairs={{0,4},{1,5},{2,6},{3,7},{4,8},{5,9},{6,10},{7,11},{8,12},{9,13},{1... | collective-permute-start | bytes 884744 | tf_op jit(solution)/shard_map/ppermute | solution.py:22
  78.8 1.7 %collective-permute-start.22 = (bf16[128,1152]{1,0:T(8,128)(2,1)S(1)}, bf16[128,1152]{1,0:T(8,128)(2,1)S(1)}, u32[]{:S(2)}, u32[]{:S(2)}) collective-permute-start(bf16[128,1152]{1,0:T(8,128)(2,1)S(1)} %get-tuple-element.15), channel_id=1, source_target_pairs={{0,12},{1,13},{2,14},{3,15},{4,0},{5,1},{6,2},{7,3},{8,4},{9,5},{1... | collective-permute-start | bytes 884744 | tf_op jit(solution)/shard_map/ppermute | solution.py:22
  80.5 0.1 slice.196
  80.7 1.3 collective-permute-start.26
  82.0 0.1 fusion.25
  82.1 2.5 %collective-permute-start.18 = (bf16[128,1152]{1,0:T(8,128)(2,1)S(1)}, bf16[128,1152]{1,0:T(8,128)(2,1)S(1)}, u32[]{:S(2)}, u32[]{:S(2)}) collective-permute-start(bf16[128,1152]{1,0:T(8,128)(2,1)S(1)} %get-tuple-element.14), channel_id=1, source_target_pairs={{0,112},{1,17},{2,114},{3,19},{4,116},{5,21},{6,118},{7,23},{8,120... | collective-permute-start | bytes 884744 | tf_op jit(solution)/shard_map/ppermute | solution.py:22
  84.7 1.2 collective-permute-start.19
  85.9 7.7 %collective-permute-done.23 = bf16[128,1152]{1,0:T(8,128)(2,1)S(1)} collective-permute-done((bf16[128,1152]{1,0:T(8,128)(2,1)S(1)}, bf16[128,1152]{1,0:T(8,128)(2,1)S(1)}, u32[]{:S(2)}, u32[]{:S(2)}) %collective-permute-start.23) | collective-permute-done | bytes 294944 | tf_op jit(solution)/shard_map/ppermute | solution.py:22
  93.6 0.1 fusion.20
  93.8 3.8 %collective-permute-start.30 = (bf16[128,1152]{1,0:T(8,128)(2,1)S(1)}, bf16[128,1152]{1,0:T(8,128)(2,1)S(1)}, u32[]{:S(2)}, u32[]{:S(2)}) collective-permute-start(bf16[128,1152]{1,0:T(8,128)(2,1)S(1)} %fusion.20), channel_id=1, source_target_pairs={{128,130},{129,131},{130,128},{131,129},{132,134},{133,135},{134,1... | collective-permute-start | bytes 884744 | tf_op jit(solution)/shard_map/ppermute | solution.py:22
  97.6 2.4 %collective-permute-start.17 = (bf16[128,1152]{1,0:T(8,128)(2,1)S(1)}, bf16[128,1152]{1,0:T(8,128)(2,1)S(1)}, u32[]{:S(2)}, u32[]{:S(2)}) collective-permute-start(bf16[128,1152]{1,0:T(8,128)(2,1)S(1)} %get-tuple-element.13), channel_id=1, source_target_pairs={{0,112},{1,17},{2,114},{3,19},{4,116},{5,21},{6,118},{7,23},{8,120... | collective-permute-start | bytes 884744 | tf_op jit(solution)/shard_map/ppermute | solution.py:22
  99.9 0.2 fusion.24
  100.1 0.1 collective-permute-start.20
  100.2 0.3 fusion.36
  100.5 5.6 %collective-permute-done.17 = bf16[128,1152]{1,0:T(8,128)(2,1)S(1)} collective-permute-done((bf16[128,1152]{1,0:T(8,128)(2,1)S(1)}, bf16[128,1152]{1,0:T(8,128)(2,1)S(1)}, u32[]{:S(2)}, u32[]{:S(2)}) %collective-permute-start.17) | collective-permute-done | bytes 294944 | tf_op jit(solution)/shard_map/ppermute | solution.py:22
  106.0 3.9 %collective-permute-done.20 = bf16[128,1152]{1,0:T(8,128)(2,1)S(1)} collective-permute-done((bf16[128,1152]{1,0:T(8,128)(2,1)S(1)}, bf16[128,1152]{1,0:T(8,128)(2,1)S(1)}, u32[]{:S(2)}, u32[]{:S(2)}) %collective-permute-start.20) | collective-permute-done | bytes 294944 | tf_op jit(solution)/shard_map/ppermute | solution.py:22
  109.9 0.1 fusion.35
  110.0 4.4 %collective-permute-start.21 = (bf16[128,1152]{1,0:T(8,128)(2,1)S(1)}, bf16[128,1152]{1,0:T(8,128)(2,1)S(1)}, u32[]{:S(2)}, u32[]{:S(2)}) collective-permute-start(bf16[128,1152]{1,0:T(8,128)(2,1)S(1)} %fusion.35), channel_id=1, source_target_pairs={{0,1},{1,0},{2,3},{3,2},{4,5},{5,4},{6,7},{7,6},{8,9},{9,8},{10,11... | collective-permute-start | bytes 884744 | tf_op jit(solution)/shard_map/ppermute | solution.py:22
  114.5 0.1 collective-permute-start.29
  114.6 1.1 collective-permute-start.28
  115.7 0.4 collective-permute-start.27
  116.1 0.2 fusion.28
  116.3 1.9 %collective-permute-start.25 = (bf16[128,1152]{1,0:T(8,128)(2,1)S(1)}, bf16[128,1152]{1,0:T(8,128)(2,1)S(1)}, u32[]{:S(2)}, u32[]{:S(2)}) collective-permute-start(bf16[128,1152]{1,0:T(8,128)(2,1)S(1)} %fusion.28), channel_id=1, source_target_pairs={{0,130},{1,129},{2,128},{3,131},{4,134},{5,133},{6,132},{7,135},{8... | collective-permute-start | bytes 884744 | tf_op jit(solution)/shard_map/ppermute | solution.py:22
  118.2 6.4 %collective-permute-done.29 = bf16[128,1152]{1,0:T(8,128)(2,1)S(1)} collective-permute-done((bf16[128,1152]{1,0:T(8,128)(2,1)S(1)}, bf16[128,1152]{1,0:T(8,128)(2,1)S(1)}, u32[]{:S(2)}, u32[]{:S(2)}) %collective-permute-start.29) | collective-permute-done | bytes 294944 | tf_op jit(solution)/shard_map/ppermute | solution.py:22
  124.7 4.9 %collective-permute-done.28 = bf16[128,1152]{1,0:T(8,128)(2,1)S(1)} collective-permute-done((bf16[128,1152]{1,0:T(8,128)(2,1)S(1)}, bf16[128,1152]{1,0:T(8,128)(2,1)S(1)}, u32[]{:S(2)}, u32[]{:S(2)}) %collective-permute-start.28) | collective-permute-done | bytes 294944 | tf_op jit(solution)/shard_map/ppermute | solution.py:22
  129.5 1.8 %collective-permute-done.27 = bf16[128,1152]{1,0:T(8,128)(2,1)S(1)} collective-permute-done((bf16[128,1152]{1,0:T(8,128)(2,1)S(1)}, bf16[128,1152]{1,0:T(8,128)(2,1)S(1)}, u32[]{:S(2)}, u32[]{:S(2)}) %collective-permute-start.27) | collective-permute-done | bytes 294944 | tf_op jit(solution)/shard_map/ppermute | solution.py:22
  131.3 1.2 fusion.8
  (59 shorter events, 1.5 us)
Async XLA Ops:
  0.0 3.2 %copy-start = (bf16[1,1152,1152]{2,1,0:T(8,128)(2,1)S(1)}, bf16[1,1152,1152]{2,1,0:T(8,128)(2,1)}, u32[]{:S(2)}) copy-start(bf16[1,1152,1152]{2,1,0:T(8,128)(2,1)} %param.11) | copy-start | bytes 7962628
  1.2 9.5 %copy-start.1 = (s32[8]{0:T(128)S(1)}, s32[8]{0:T(128)}, u32[]{:S(2)}) copy-start(s32[8]{0:T(128)} %constant.47.clone) | copy-start | bytes 100
  1.3 9.5 %copy-start.2 = (s32[8]{0:T(128)S(1)}, s32[8]{0:T(128)}, u32[]{:S(2)}) copy-start(s32[8]{0:T(128)} %constant.46.clone) | copy-start | bytes 100
  1.3 10.4 %copy-start.3 = (s32[8]{0:T(128)S(1)}, s32[8]{0:T(128)}, u32[]{:S(2)}) copy-start(s32[8]{0:T(128)} %constant.45.clone) | copy-start | bytes 100
  5.0 7.6 %collective-permute-start = (bf16[128,1152]{1,0:T(8,128)(2,1)S(1)}, bf16[128,1152]{1,0:T(8,128)(2,1)}, u32[]{:S(2)}, u32[]{:S(2)}) collective-permute-start(bf16[128,1152]{1,0:T(8,128)(2,1)S(1)} %multiply_convert_fusion), channel_id=1, source_target_pairs={{1,129},{3,131},{5,133},{7,135},{9,137},{11,139},{13,141},{15,143}... | collective-permute-start | bytes 884744 | tf_op jit(solution)/shard_map/ppermute | solution.py:22
  7.2 11.9 %collective-permute-start.14 = (bf16[128,1152]{1,0:T(8,128)(2,1)S(1)}, bf16[128,1152]{1,0:T(8,128)(2,1)}, u32[]{:S(2)}, u32[]{:S(2)}) collective-permute-start(bf16[128,1152]{1,0:T(8,128)(2,1)S(1)} %multiply_convert_fusion), channel_id=1, source_target_pairs={{0,8},{1,9},{2,10},{3,11},{4,12},{5,13},{6,14},{7,15},{8,0},{9,1},... | collective-permute-start | bytes 884744 | tf_op jit(solution)/shard_map/ppermute | solution.py:22
  9.3 14.7 %collective-permute-start.13 = (bf16[128,1152]{1,0:T(8,128)(2,1)S(1)}, bf16[128,1152]{1,0:T(8,128)(2,1)}, u32[]{:S(2)}, u32[]{:S(2)}) collective-permute-start(bf16[128,1152]{1,0:T(8,128)(2,1)S(1)} %multiply_convert_fusion), channel_id=1, source_target_pairs={{0,12},{1,13},{2,14},{3,15},{4,0},{5,1},{6,2},{7,3},{8,4},{9,5},{1... | collective-permute-start | bytes 884744 | tf_op jit(solution)/shard_map/ppermute | solution.py:22
  10.4 13.7 %collective-permute-start.12 = (bf16[128,1152]{1,0:T(8,128)(2,1)S(1)}, bf16[128,1152]{1,0:T(8,128)(2,1)}, u32[]{:S(2)}, u32[]{:S(2)}) collective-permute-start(bf16[128,1152]{1,0:T(8,128)(2,1)S(1)} %multiply_convert_fusion), channel_id=1, source_target_pairs={{0,4},{1,5},{2,6},{3,7},{4,8},{5,9},{6,10},{7,11},{8,12},{9,13},{1... | collective-permute-start | bytes 884744 | tf_op jit(solution)/shard_map/ppermute | solution.py:22
  14.4 15.8 %collective-permute-start.1 = (bf16[128,1152]{1,0:T(8,128)(2,1)}, bf16[128,1152]{1,0:T(8,128)(2,1)S(1)}, u32[]{:S(2)}, u32[]{:S(2)}) collective-permute-start(bf16[128,1152]{1,0:T(8,128)(2,1)} %broadcast_select_fusion.2), channel_id=1, source_target_pairs={{0,1},{1,0},{2,3},{3,2},{4,5},{5,4},{6,7},{7,6},{8,9},{9,8},{10,11... | collective-permute-start | bytes 884744 | tf_op jit(solution)/shard_map/ppermute | solution.py:22
  25.3 34.5 %collective-permute-start.15 = (bf16[512,1152]{1,0:T(8,128)(2,1)S(1)}, bf16[512,1152]{1,0:T(8,128)(2,1)S(1)}, u32[]{:S(2)}, u32[]{:S(2)}) collective-permute-start(bf16[512,1152]{1,0:T(8,128)(2,1)S(1)} %pad_maximum_fusion), channel_id=1, source_target_pairs={{128,0},{129,3},{130,2},{131,1},{132,4},{133,7},{134,6},{135,5},{1... | collective-permute-start | bytes 3538952 | tf_op jit(solution)/shard_map/ppermute | solution.py:22
  29.0 8.0 %collective-permute-start.8 = (bf16[128,1152]{1,0:T(8,128)(2,1)}, bf16[128,1152]{1,0:T(8,128)(2,1)S(1)}, u32[]{:S(2)}, u32[]{:S(2)}) collective-permute-start(bf16[128,1152]{1,0:T(8,128)(2,1)} %collective-permute-done), channel_id=1, source_target_pairs={{0,128},{1,131},{2,130},{3,129},{4,132},{5,135},{6,134},{7,133},{8... | collective-permute-start | bytes 884744 | tf_op jit(solution)/shard_map/ppermute | solution.py:22
  31.3 7.3 %collective-permute-start.2 = (bf16[128,1152]{1,0:T(8,128)(2,1)S(1)}, bf16[128,1152]{1,0:T(8,128)(2,1)S(1)}, u32[]{:S(2)}, u32[]{:S(2)}) collective-permute-start(bf16[128,1152]{1,0:T(8,128)(2,1)S(1)} %broadcast_select_fusion), channel_id=1, source_target_pairs={{0,16},{1,113},{2,18},{3,115},{4,20},{5,117},{6,22},{7,119},{8,24}... | collective-permute-start | bytes 884744 | tf_op jit(solution)/shard_map/ppermute | solution.py:22
  31.4 11.8 %collective-permute-start.3 = (bf16[128,1152]{1,0:T(8,128)(2,1)S(1)}, bf16[128,1152]{1,0:T(8,128)(2,1)S(1)}, u32[]{:S(2)}, u32[]{:S(2)}) collective-permute-start(bf16[128,1152]{1,0:T(8,128)(2,1)S(1)} %broadcast_select_fusion), channel_id=1, source_target_pairs={{0,32},{1,97},{2,34},{3,99},{4,36},{5,101},{6,38},{7,103},{8,40},{... | collective-permute-start | bytes 884744 | tf_op jit(solution)/shard_map/ppermute | solution.py:22
  37.0 8.1 %collective-permute-start.9 = (bf16[128,1152]{1,0:T(8,128)(2,1)S(1)}, bf16[128,1152]{1,0:T(8,128)(2,1)S(1)}, u32[]{:S(2)}, u32[]{:S(2)}) collective-permute-start(bf16[128,1152]{1,0:T(8,128)(2,1)S(1)} %get-tuple-element.12), channel_id=1, source_target_pairs={{0,4},{1,5},{2,6},{3,7},{4,8},{5,9},{6,10},{7,11},{8,12},{9,13},{1... | collective-permute-start | bytes 884744 | tf_op jit(solution)/shard_map/ppermute | solution.py:22
  38.4 7.9 %collective-permute-start.10 = (bf16[128,1152]{1,0:T(8,128)(2,1)S(1)}, bf16[128,1152]{1,0:T(8,128)(2,1)S(1)}, u32[]{:S(2)}, u32[]{:S(2)}) collective-permute-start(bf16[128,1152]{1,0:T(8,128)(2,1)S(1)} %get-tuple-element.12), channel_id=1, source_target_pairs={{0,12},{1,13},{2,14},{3,15},{4,0},{5,1},{6,2},{7,3},{8,4},{9,5},{1... | collective-permute-start | bytes 884744 | tf_op jit(solution)/shard_map/ppermute | solution.py:22
  38.6 14.6 %collective-permute-start.11 = (bf16[128,1152]{1,0:T(8,128)(2,1)S(1)}, bf16[128,1152]{1,0:T(8,128)(2,1)S(1)}, u32[]{:S(2)}, u32[]{:S(2)}) collective-permute-start(bf16[128,1152]{1,0:T(8,128)(2,1)S(1)} %get-tuple-element.12), channel_id=1, source_target_pairs={{0,8},{1,9},{2,10},{3,11},{4,12},{5,13},{6,14},{7,15},{8,0},{9,1},... | collective-permute-start | bytes 884744 | tf_op jit(solution)/shard_map/ppermute | solution.py:22
  43.3 16.4 %collective-permute-start.4 = (bf16[256,1152]{1,0:T(8,128)(2,1)S(1)}, bf16[256,1152]{1,0:T(8,128)(2,1)S(1)}, u32[]{:S(2)}, u32[]{:S(2)}) collective-permute-start(bf16[256,1152]{1,0:T(8,128)(2,1)S(1)} %pad_maximum_fusion.2), channel_id=1, source_target_pairs={{0,1},{1,0},{2,3},{3,2},{4,5},{5,4},{6,7},{7,6},{8,9},{9,8},{10,11... | collective-permute-start | bytes 1769480 | tf_op jit(solution)/shard_map/ppermute | solution.py:22
  45.1 8.1 %collective-permute-start.6 = (bf16[64,1152]{1,0:T(8,128)(2,1)S(1)}, bf16[64,1152]{1,0:T(8,128)(2,1)S(1)}, u32[]{:S(2)}, u32[]{:S(2)}) collective-permute-start(bf16[64,1152]{1,0:T(8,128)(2,1)S(1)} %slice_select_fusion), channel_id=1, source_target_pairs={{0,32},{1,97},{2,34},{3,99},{4,36},{5,101},{6,38},{7,103},{8,40},{... | collective-permute-start | bytes 442376 | tf_op jit(solution)/shard_map/ppermute | solution.py:22
  46.3 9.6 %collective-permute-start.5 = (bf16[128,1152]{1,0:T(8,128)(2,1)S(1)}, bf16[128,1152]{1,0:T(8,128)(2,1)S(1)}, u32[]{:S(2)}, u32[]{:S(2)}) collective-permute-start(bf16[128,1152]{1,0:T(8,128)(2,1)S(1)} %collective-permute-done.3), channel_id=1, source_target_pairs={{0,16},{1,113},{2,18},{3,115},{4,20},{5,117},{6,22},{7,119},{8,24}... | collective-permute-start | bytes 884744 | tf_op jit(solution)/shard_map/ppermute | solution.py:22
  55.9 5.4 %collective-permute-start.7 = (bf16[192,1152]{1,0:T(8,128)(2,1)S(1)}, bf16[192,1152]{1,0:T(8,128)(2,1)S(1)}, u32[]{:S(2)}, u32[]{:S(2)}) collective-permute-start(bf16[192,1152]{1,0:T(8,128)(2,1)S(1)} %pad_maximum_fusion.3), channel_id=1, source_target_pairs={{0,1},{1,0},{2,3},{3,2},{4,5},{5,4},{6,7},{7,6},{8,9},{9,8},{10,11... | collective-permute-start | bytes 1327112 | tf_op jit(solution)/shard_map/ppermute | solution.py:22
  68.6 13.4 %collective-permute-start.16 = (bf16[448,1152]{1,0:T(8,128)(2,1)S(1)}, bf16[448,1152]{1,0:T(8,128)(2,1)S(1)}, u32[]{:S(2)}, u32[]{:S(2)}) collective-permute-start(bf16[448,1152]{1,0:T(8,128)(2,1)S(1)} %pad_maximum_fusion.1), channel_id=1, source_target_pairs={{0,1},{1,0},{2,3},{3,2},{4,5},{5,4},{6,7},{7,6},{8,9},{9,8},{10,11... | collective-permute-start | bytes 3096584 | tf_op jit(solution)/shard_map/ppermute | solution.py:22
  71.9 12.8 %collective-permute-start.24 = (bf16[128,1152]{1,0:T(8,128)(2,1)S(1)}, bf16[128,1152]{1,0:T(8,128)(2,1)S(1)}, u32[]{:S(2)}, u32[]{:S(2)}) collective-permute-start(bf16[128,1152]{1,0:T(8,128)(2,1)S(1)} %get-tuple-element.16), channel_id=1, source_target_pairs={{0,8},{1,9},{2,10},{3,11},{4,12},{5,13},{6,14},{7,15},{8,0},{9,1},... | collective-permute-start | bytes 884744 | tf_op jit(solution)/shard_map/ppermute | solution.py:22
  76.2 17.4 %collective-permute-start.23 = (bf16[128,1152]{1,0:T(8,128)(2,1)S(1)}, bf16[128,1152]{1,0:T(8,128)(2,1)S(1)}, u32[]{:S(2)}, u32[]{:S(2)}) collective-permute-start(bf16[128,1152]{1,0:T(8,128)(2,1)S(1)} %get-tuple-element.17), channel_id=1, source_target_pairs={{0,4},{1,5},{2,6},{3,7},{4,8},{5,9},{6,10},{7,11},{8,12},{9,13},{1... | collective-permute-start | bytes 884744 | tf_op jit(solution)/shard_map/ppermute | solution.py:22
  78.8 14.8 %collective-permute-start.22 = (bf16[128,1152]{1,0:T(8,128)(2,1)S(1)}, bf16[128,1152]{1,0:T(8,128)(2,1)S(1)}, u32[]{:S(2)}, u32[]{:S(2)}) collective-permute-start(bf16[128,1152]{1,0:T(8,128)(2,1)S(1)} %get-tuple-element.15), channel_id=1, source_target_pairs={{0,12},{1,13},{2,14},{3,15},{4,0},{5,1},{6,2},{7,3},{8,4},{9,5},{1... | collective-permute-start | bytes 884744 | tf_op jit(solution)/shard_map/ppermute | solution.py:22
  80.7 19.5 %collective-permute-start.26 = (bf16[512,1152]{1,0:T(8,128)(2,1)S(1)}, bf16[512,1152]{1,0:T(8,128)(2,1)S(1)}, u32[]{:S(2)}, u32[]{:S(2)}) collective-permute-start(bf16[512,1152]{1,0:T(8,128)(2,1)S(1)} %slice.196), channel_id=1, source_target_pairs={{0,128},{1,131},{2,130},{3,129},{4,132},{5,135},{6,134},{7,133},{8... | collective-permute-start | bytes 3538952 | tf_op jit(solution)/shard_map/ppermute | solution.py:22
  82.1 17.8 %collective-permute-start.18 = (bf16[128,1152]{1,0:T(8,128)(2,1)S(1)}, bf16[128,1152]{1,0:T(8,128)(2,1)S(1)}, u32[]{:S(2)}, u32[]{:S(2)}) collective-permute-start(bf16[128,1152]{1,0:T(8,128)(2,1)S(1)} %get-tuple-element.14), channel_id=1, source_target_pairs={{0,112},{1,17},{2,114},{3,19},{4,116},{5,21},{6,118},{7,23},{8,120... | collective-permute-start | bytes 884744 | tf_op jit(solution)/shard_map/ppermute | solution.py:22
  84.7 15.2 %collective-permute-start.19 = (bf16[64,1152]{1,0:T(8,128)(2,1)S(1)}, bf16[64,1152]{1,0:T(8,128)(2,1)S(1)}, u32[]{:S(2)}, u32[]{:S(2)}) collective-permute-start(bf16[64,1152]{1,0:T(8,128)(2,1)S(1)} %add_convert_fusion), channel_id=1, source_target_pairs={{0,96},{1,33},{2,98},{3,35},{4,100},{5,37},{6,102},{7,39},{8,104},... | collective-permute-start | bytes 442376 | tf_op jit(solution)/shard_map/ppermute | solution.py:22
  93.8 24.5 %collective-permute-start.30 = (bf16[128,1152]{1,0:T(8,128)(2,1)S(1)}, bf16[128,1152]{1,0:T(8,128)(2,1)S(1)}, u32[]{:S(2)}, u32[]{:S(2)}) collective-permute-start(bf16[128,1152]{1,0:T(8,128)(2,1)S(1)} %fusion.20), channel_id=1, source_target_pairs={{128,130},{129,131},{130,128},{131,129},{132,134},{133,135},{134,1... | collective-permute-start | bytes 884744 | tf_op jit(solution)/shard_map/ppermute | solution.py:22
  97.6 8.5 %collective-permute-start.17 = (bf16[128,1152]{1,0:T(8,128)(2,1)S(1)}, bf16[128,1152]{1,0:T(8,128)(2,1)S(1)}, u32[]{:S(2)}, u32[]{:S(2)}) collective-permute-start(bf16[128,1152]{1,0:T(8,128)(2,1)S(1)} %get-tuple-element.13), channel_id=1, source_target_pairs={{0,112},{1,17},{2,114},{3,19},{4,116},{5,21},{6,118},{7,23},{8,120... | collective-permute-start | bytes 884744 | tf_op jit(solution)/shard_map/ppermute | solution.py:22
  100.1 9.8 %collective-permute-start.20 = (bf16[128,1152]{1,0:T(8,128)(2,1)S(1)}, bf16[128,1152]{1,0:T(8,128)(2,1)S(1)}, u32[]{:S(2)}, u32[]{:S(2)}) collective-permute-start(bf16[128,1152]{1,0:T(8,128)(2,1)S(1)} %fusion.24), channel_id=1, source_target_pairs={{0,96},{1,33},{2,98},{3,35},{4,100},{5,37},{6,102},{7,39},{8,104},... | collective-permute-start | bytes 884744 | tf_op jit(solution)/shard_map/ppermute | solution.py:22
  110.0 6.1 %collective-permute-start.21 = (bf16[128,1152]{1,0:T(8,128)(2,1)S(1)}, bf16[128,1152]{1,0:T(8,128)(2,1)S(1)}, u32[]{:S(2)}, u32[]{:S(2)}) collective-permute-start(bf16[128,1152]{1,0:T(8,128)(2,1)S(1)} %fusion.35), channel_id=1, source_target_pairs={{0,1},{1,0},{2,3},{3,2},{4,5},{5,4},{6,7},{7,6},{8,9},{9,8},{10,11... | collective-permute-start | bytes 884744 | tf_op jit(solution)/shard_map/ppermute | solution.py:22
  114.5 10.2 %collective-permute-start.29 = (bf16[128,1152]{1,0:T(8,128)(2,1)S(1)}, bf16[128,1152]{1,0:T(8,128)(2,1)S(1)}, u32[]{:S(2)}, u32[]{:S(2)}) collective-permute-start(bf16[128,1152]{1,0:T(8,128)(2,1)S(1)} %get-tuple-element.19), channel_id=1, source_target_pairs={{0,8},{1,9},{2,10},{3,11},{4,12},{5,13},{6,14},{7,15},{8,0},{9,1},... | collective-permute-start | bytes 884744 | tf_op jit(solution)/shard_map/ppermute | solution.py:22
  114.6 14.9 %collective-permute-start.28 = (bf16[128,1152]{1,0:T(8,128)(2,1)S(1)}, bf16[128,1152]{1,0:T(8,128)(2,1)S(1)}, u32[]{:S(2)}, u32[]{:S(2)}) collective-permute-start(bf16[128,1152]{1,0:T(8,128)(2,1)S(1)} %get-tuple-element.20), channel_id=1, source_target_pairs={{0,4},{1,5},{2,6},{3,7},{4,8},{5,9},{6,10},{7,11},{8,12},{9,13},{1... | collective-permute-start | bytes 884744 | tf_op jit(solution)/shard_map/ppermute | solution.py:22
  115.7 15.6 %collective-permute-start.27 = (bf16[128,1152]{1,0:T(8,128)(2,1)S(1)}, bf16[128,1152]{1,0:T(8,128)(2,1)S(1)}, u32[]{:S(2)}, u32[]{:S(2)}) collective-permute-start(bf16[128,1152]{1,0:T(8,128)(2,1)S(1)} %get-tuple-element.18), channel_id=1, source_target_pairs={{0,12},{1,13},{2,14},{3,15},{4,0},{5,1},{6,2},{7,3},{8,4},{9,5},{1... | collective-permute-start | bytes 884744 | tf_op jit(solution)/shard_map/ppermute | solution.py:22
  116.3 15.0 %collective-permute-start.25 = (bf16[128,1152]{1,0:T(8,128)(2,1)S(1)}, bf16[128,1152]{1,0:T(8,128)(2,1)S(1)}, u32[]{:S(2)}, u32[]{:S(2)}) collective-permute-start(bf16[128,1152]{1,0:T(8,128)(2,1)S(1)} %fusion.28), channel_id=1, source_target_pairs={{0,130},{1,129},{2,128},{3,131},{4,134},{5,133},{6,132},{7,135},{8... | collective-permute-start | bytes 884744 | tf_op jit(solution)/shard_map/ppermute | solution.py:22
where the time goes:
time: 133 us
  waiting for transfers between devices  53.5 us (40%)
  starting transfers between devices  51.7 us (39%)
  other arithmetic  11.8 us (9%)
  matrix products  11.6 us (9%)
  local copies, waits for them, and re-layouts  2.09 us (2%)
  between operations  1.77 us (1%)
    ppermute x31, waiting for transfers between devices, hop(): return lax.ppermute(value, ('tower', 'blk'), pairs)  53.5 us
    ppermute x31, starting transfers between devices, hop(): return lax.ppermute(value, ('tower', 'blk'), pairs)  51.7 us
    dot_general x1, matrix products, pair_coef(): lax.dot_general(image_rows, text_rows, (((1,), (1,)), ((), ())), preferre...  4.09 us
    dot_general x1, matrix products, tile(): lax.dot_general(coef, image_rows, (((0,), (0,)), ((), ())), preferred_ele...  2.98 us
    dot_general x1, matrix products, tile(): image_part = jnp.dot(coef, text_rows, preferred_element_type=f32)  2.88 us
  transfers between devices with their start and end apart: 31, of which 13 were waited for; matrix products, arithmetic and copies ran while one was open for 9% of the time, Pallas kernels for 0%

commit v1 on v0

--- a/solution.py
+++ b/solution.py
@@ -1,6 +1,8 @@
 import jax
 import jax.numpy as jnp
 from jax import lax
+from jax.experimental import pallas as pl
+from jax.experimental.pallas import tpu as pltpu
 from jax.sharding import PartitionSpec as P
 
 
@@ -22,14 +24,56 @@
     return lax.ppermute(value, ("tower", "blk"), pairs)
 
 
-def embed_rows(feats, gain, weight):
-    values = feats.astype(jnp.float32)
+COLUMN_CUTS = 1
+
+
+def embed_kernel(feats_hbm, gain_hbm, weight, out, feats, gain, staged, head, sems):
+    cut = staged.shape[2]
+    ahead = [
+        pltpu.make_async_copy(feats_hbm.at[0], feats, sems.at[COLUMN_CUTS]),
+        pltpu.make_async_copy(gain_hbm, gain, sems.at[COLUMN_CUTS + 1]),
+    ]
+    copies = [
+        pltpu.make_async_copy(weight.at[0, :, pl.ds(k * cut, cut)], staged.at[k], sems.at[k])
+        for k in range(COLUMN_CUTS)
+    ]
+    for copy in ahead + copies:
+        copy.start()
+    for copy in ahead:
+        copy.wait()
+    values = feats[...].astype(jnp.float32)
     center = values - jnp.mean(values, axis=-1, keepdims=True)
     spread = jnp.mean(center * center, axis=-1, keepdims=True)
-    normed = (center * lax.rsqrt(spread + 1e-06) * gain).astype(jnp.bfloat16)
-    head = jnp.dot(normed, weight, preferred_element_type=jnp.float32)
-    length = jnp.sum(head * head, axis=-1, keepdims=True)
-    return (head * lax.rsqrt(length + 1e-06)).astype(jnp.bfloat16)
+    normed = (center * lax.rsqrt(spread + 1e-06) * gain[...]).astype(jnp.bfloat16)
+    length = jnp.zeros((values.shape[0], 1), jnp.float32)
+    for k, copy in enumerate(copies):
+        copy.wait()
+        part = jnp.dot(normed, staged[k], preferred_element_type=jnp.float32)
+        length = length + jnp.sum(part * part, axis=-1, keepdims=True)
+        head[k] = part
+    factor = lax.rsqrt(length + 1e-06)
+    for k in range(COLUMN_CUTS):
+        out[:, k * cut : (k + 1) * cut] = (head[k] * factor).astype(jnp.bfloat16)
+
+
+def embed_rows(feats, gain, weight):
+    _, ex, width = feats.shape
+    cut = width // COLUMN_CUTS
+    return pl.pallas_call(
+        embed_kernel,
+        out_shape=jax.ShapeDtypeStruct((ex, width), jnp.bfloat16),
+        in_specs=[pl.BlockSpec(memory_space=pltpu.HBM)] * 3,
+        out_specs=pl.BlockSpec(memory_space=pltpu.VMEM),
+        scratch_shapes=[
+            pltpu.VMEM((ex, width), jnp.bfloat16),
+            pltpu.VMEM((1, width), jnp.float32),
+            pltpu.VMEM((COLUMN_CUTS, width, cut), jnp.bfloat16),
+            pltpu.VMEM((COLUMN_CUTS, ex, cut), jnp.float32),
+            pltpu.SemaphoreType.DMA((COLUMN_CUTS + 2,)),
+        ],
+        compiler_params=pltpu.CompilerParams(vmem_limit_bytes=66_400_000),
+        name="embed",
+    )(feats, gain, weight)
 
 
 def pair_coef(image_rows, text_rows, image_ids, text_ids, scale, shift):
@@ -117,7 +161,12 @@
     below = hop(send[:ex], down_y)
     above = hop(send[ex : 2 * ex], up_y)
     far = hop(send[2 * ex :], two_y)
-    return part[:ex] + below.astype(jnp.float32) + above.astype(jnp.float32) + far.astype(jnp.float32)
+    return (
+        part[:ex]
+        + below.astype(jnp.float32)
+        + above.astype(jnp.float32)
+        + far.astype(jnp.float32)
+    )
 
 
 def pick(table, order, size):
@@ -127,7 +176,7 @@
 
 def tile(pooled, final_gain, head_weight, pair_ids, log_scale, bias):
     bf16, f32 = jnp.bfloat16, jnp.float32
-    local = embed_rows(pooled[0], final_gain[0], head_weight[0])
+    local = embed_rows(pooled, final_gain, head_weight)
     ex = local.shape[0]
     half = ex // 2
     scale = jnp.exp(log_scale[0])
@@ -191,11 +240,14 @@
     r4 = hop((mine(part[7]) + got[3 * ex :]).astype(bf16), unring2_z)
     r1 = hop((part[1] + got[:ex]).astype(bf16), unring_z)
     r2 = part[2] + got[ex : 2 * ex].astype(f32) + r3.astype(f32) + whole(r4, jnp.zeros_like(r4))
-    r2 = hop(r2.astype(bf16), unring2_z)
+    r2_send = r2.astype(bf16)
+    r2 = hop(r2_send, unring2_z)
     image_sum = part[0] + r1.astype(f32) + r2.astype(f32)
 
     column_part = text_part[NY * ex :]
-    column_part = column_part + hop(column_part.astype(bf16), from_column)
+    came = hop(column_part.astype(bf16), from_column)
+    column_part, _ = lax.optimization_barrier((column_part, r2_send))
+    column_part = column_part + came
     spread_sum = collect_y(text_part[: NY * ex], ex)
     text_sum = collect_y(column_part, ex)
     spread_sum = lax.optimization_barrier(spread_sum.astype(bf16))

time: 133 us -> 131 us (0.985)
  other arithmetic: 11.8 us -> 4.36 us
  waiting for transfers between devices: 53.5 us -> 58.1 us
  Pallas kernels: 0 us -> 3.36 us
  matrix products: 11.6 us -> 9.95 us
    ppermute x31, waiting for transfers between devices: 53.5 us -> 58.1 us  [hop(): return lax.ppermute(value, ('tower', 'blk'), pairs)]
    pallas_call x0 -> x1, Pallas kernels: none -> 3.36 us  [embed_rows(): pl.pallas_call(embed_kernel, out_shape=jax.ShapeDtypeStruct((ex, width),...]
    reduce_sum x2 -> x0, other arithmetic: 2.43 us -> none  [the longest x1 1.23 us: embed_rows(): center = values - jnp.mean(values, axis=-1, keepdims=True)]
    select_n x1, other arithmetic: 1.82 us -> 0.04 us  [tile(): kept = jnp.where(image_side, local, near)]
    dot_general x1 -> x0, matrix products: 1.7 us -> none  [embed_rows(): head = jnp.dot(normed, weight, preferred_element_type=jnp.float32)]
  transfers between devices with their start and end apart: 31 -> 31, of which waited for: 13 -> 16; matrix products, arithmetic and copies ran while one was open for 9% -> 5% of each run, Pallas kernels for 0% -> 0%
where the time goes in v1:
time: 131 us
  waiting for transfers between devices  58.1 us (44%)
  starting transfers between devices  52.5 us (40%)
  matrix products  9.95 us (8%)
  other arithmetic  4.36 us (3%)
  Pallas kernels  3.36 us (3%)
  between operations  1.78 us (1%)
    ppermute x31, waiting for transfers between devices, hop(): return lax.ppermute(value, ('tower', 'blk'), pairs)  58.1 us
    ppermute x31, starting transfers between devices, hop(): return lax.ppermute(value, ('tower', 'blk'), pairs)  52.5 us
    dot_general x1, matrix products, pair_coef(): lax.dot_general(image_rows, text_rows, (((1,), (1,)), ((), ())), preferre...  4.09 us
    pallas_call x1, Pallas kernels, embed_rows(): pl.pallas_call(embed_kernel, out_shape=jax.ShapeDtypeStruct((ex, width),...  3.36 us
    dot_general x1, matrix products, tile(): lax.dot_general(coef, image_rows, (((0,), (0,)), ((), ())), preferred_ele...  2.98 us
    dot_general x1, matrix products, tile(): image_part = jnp.dot(coef, text_rows, preferred_element_type=f32)  2.88 us
  transfers between devices with their start and end apart: 31, of which 16 were waited for; matrix products, arithmetic and copies ran while one was open for 5% of the time, Pallas kernels for 0%

profile of v1, /device:TPU:107, one launch (start us, length us, event | category | flops | bytes accessed | tf_op | source)
XLA Modules:
  0.0 130.9 jit_solution(3678179170879731024)
XLA Ops:
  0.0 3.4 %embed.1 = bf16[128,1152]{1,0:T(8,128)(2,1)} custom-call(bf16[1,128,1152]{2,1,0:T(8,128)(2,1)} %feats_hbm.1, f32[1,1152]{1,0:T(1,128)} %gain_hbm.1, bf16[1,1152,1152]{2,1,0:T(8,128)(2,1)} %weight.1), custom_call_target="tpu_custom_call" | custom-call | tf_op jit(solution)/shard_map/embed/pallas_call | solution.py:62
  3.4 2.2 %collective-permute-start = (bf16[128,1152]{1,0:T(8,128)(2,1)}, bf16[128,1152]{1,0:T(8,128)(2,1)S(1)}, u32[]{:S(2)}, u32[]{:S(2)}) collective-permute-start(bf16[128,1152]{1,0:T(8,128)(2,1)} %embed.1), channel_id=1, source_target_pairs={{1,129},{3,131},{5,133},{7,135},{9,137},{11,139},{13,141},{15,143}... | collective-permute-start | bytes 884744 | tf_op jit(solution)/shard_map/ppermute | solution.py:24
  5.6 2.1 %collective-permute-start.14 = (bf16[128,1152]{1,0:T(8,128)(2,1)}, bf16[128,1152]{1,0:T(8,128)(2,1)S(1)}, u32[]{:S(2)}, u32[]{:S(2)}) collective-permute-start(bf16[128,1152]{1,0:T(8,128)(2,1)} %embed.1), channel_id=1, source_target_pairs={{0,8},{1,9},{2,10},{3,11},{4,12},{5,13},{6,14},{7,15},{8,0},{9,1},... | collective-permute-start | bytes 884744 | tf_op jit(solution)/shard_map/ppermute | solution.py:24
  7.7 1.1 collective-permute-start.13
  8.7 0.4 collective-permute-start.12
  9.2 0.1 select_reduce_fusion
  9.5 1.6 %collective-permute-done = bf16[128,1152]{1,0:T(8,128)(2,1)S(1)} collective-permute-done((bf16[128,1152]{1,0:T(8,128)(2,1)}, bf16[128,1152]{1,0:T(8,128)(2,1)S(1)}, u32[]{:S(2)}, u32[]{:S(2)}) %collective-permute-start) | collective-permute-done | bytes 294944 | tf_op jit(solution)/shard_map/ppermute | solution.py:24
  11.1 1.2 collective-permute-start.1
  12.4 0.1 select_reduce_fusion.1
  13.8 0.3 collective-permute-done.14
  14.1 8.5 %collective-permute-done.13 = bf16[128,1152]{1,0:T(8,128)(2,1)S(1)} collective-permute-done((bf16[128,1152]{1,0:T(8,128)(2,1)}, bf16[128,1152]{1,0:T(8,128)(2,1)S(1)}, u32[]{:S(2)}, u32[]{:S(2)}) %collective-permute-start.13) | collective-permute-done | bytes 294944 | tf_op jit(solution)/shard_map/ppermute | solution.py:24
  22.6 1.1 pad_maximum_fusion
  23.7 3.5 %collective-permute-start.15 = (bf16[512,1152]{1,0:T(8,128)(2,1)S(1)}, bf16[512,1152]{1,0:T(8,128)(2,1)S(1)}, u32[]{:S(2)}, u32[]{:S(2)}) collective-permute-start(bf16[512,1152]{1,0:T(8,128)(2,1)S(1)} %pad_maximum_fusion), channel_id=1, source_target_pairs={{128,0},{129,3},{130,2},{131,1},{132,4},{133,7},{134,6},{135,5},{1... | collective-permute-start | bytes 3538952 | tf_op jit(solution)/shard_map/ppermute | solution.py:24
  27.2 1.3 collective-permute-start.8
  28.6 0.1 collective-permute-start.2
  28.7 0.1 collective-permute-start.3
  28.8 6.2 %collective-permute-done.8 = bf16[128,1152]{1,0:T(8,128)(2,1)S(1)} collective-permute-done((bf16[128,1152]{1,0:T(8,128)(2,1)S(1)}, bf16[128,1152]{1,0:T(8,128)(2,1)S(1)}, u32[]{:S(2)}, u32[]{:S(2)}) %collective-permute-start.8) | collective-permute-done | bytes 294944 | tf_op jit(solution)/shard_map/ppermute | solution.py:24
  35.1 1.4 %collective-permute-start.9 = (bf16[128,1152]{1,0:T(8,128)(2,1)S(1)}, bf16[128,1152]{1,0:T(8,128)(2,1)S(1)}, u32[]{:S(2)}, u32[]{:S(2)}) collective-permute-start(bf16[128,1152]{1,0:T(8,128)(2,1)S(1)} %get-tuple-element.14), channel_id=1, source_target_pairs={{0,4},{1,5},{2,6},{3,7},{4,8},{5,9},{6,10},{7,11},{8,12},{9,13},{1... | collective-permute-start | bytes 884744 | tf_op jit(solution)/shard_map/ppermute | solution.py:24
  36.4 0.2 collective-permute-start.10
  36.7 2.1 %collective-permute-start.11 = (bf16[128,1152]{1,0:T(8,128)(2,1)S(1)}, bf16[128,1152]{1,0:T(8,128)(2,1)S(1)}, u32[]{:S(2)}, u32[]{:S(2)}) collective-permute-start(bf16[128,1152]{1,0:T(8,128)(2,1)S(1)} %get-tuple-element.14), channel_id=1, source_target_pairs={{0,8},{1,9},{2,10},{3,11},{4,12},{5,13},{6,14},{7,15},{8,0},{9,1},... | collective-permute-start | bytes 884744 | tf_op jit(solution)/shard_map/ppermute | solution.py:24
  38.8 1.8 %collective-permute-done.3 = bf16[128,1152]{1,0:T(8,128)(2,1)S(1)} collective-permute-done((bf16[128,1152]{1,0:T(8,128)(2,1)S(1)}, bf16[128,1152]{1,0:T(8,128)(2,1)S(1)}, u32[]{:S(2)}, u32[]{:S(2)}) %collective-permute-start.3) | collective-permute-done | bytes 294944 | tf_op jit(solution)/shard_map/ppermute | solution.py:24
  40.6 1.6 %collective-permute-start.4 = (bf16[256,1152]{1,0:T(8,128)(2,1)S(1)}, bf16[256,1152]{1,0:T(8,128)(2,1)S(1)}, u32[]{:S(2)}, u32[]{:S(2)}) collective-permute-start(bf16[256,1152]{1,0:T(8,128)(2,1)S(1)} %pad_maximum_fusion.2), channel_id=1, source_target_pairs={{0,1},{1,0},{2,3},{3,2},{4,5},{5,4},{6,7},{7,6},{8,9},{9,8},{10,11... | collective-permute-start | bytes 1769480 | tf_op jit(solution)/shard_map/ppermute | solution.py:24
  42.3 0.9 collective-permute-done.9
  43.2 1.3 %collective-permute-start.6 = (bf16[64,1152]{1,0:T(8,128)(2,1)S(1)}, bf16[64,1152]{1,0:T(8,128)(2,1)S(1)}, u32[]{:S(2)}, u32[]{:S(2)}) collective-permute-start(bf16[64,1152]{1,0:T(8,128)(2,1)S(1)} %slice_select_fusion), channel_id=1, source_target_pairs={{0,32},{1,97},{2,34},{3,99},{4,36},{5,101},{6,38},{7,103},{8,40},{... | collective-permute-start | bytes 442376 | tf_op jit(solution)/shard_map/ppermute | solution.py:24
  44.5 0.1 collective-permute-start.5
  44.7 6.6 %collective-permute-done.11 = bf16[128,1152]{1,0:T(8,128)(2,1)S(1)} collective-permute-done((bf16[128,1152]{1,0:T(8,128)(2,1)S(1)}, bf16[128,1152]{1,0:T(8,128)(2,1)S(1)}, u32[]{:S(2)}, u32[]{:S(2)}) %collective-permute-start.11) | collective-permute-done | bytes 294944 | tf_op jit(solution)/shard_map/ppermute | solution.py:24
  51.3 2.0 %collective-permute-done.5 = bf16[128,1152]{1,0:T(8,128)(2,1)S(1)} collective-permute-done((bf16[128,1152]{1,0:T(8,128)(2,1)S(1)}, bf16[128,1152]{1,0:T(8,128)(2,1)S(1)}, u32[]{:S(2)}, u32[]{:S(2)}) %collective-permute-start.5) | collective-permute-done | bytes 294944 | tf_op jit(solution)/shard_map/ppermute | solution.py:24
  53.3 4.5 %collective-permute-start.7 = (bf16[192,1152]{1,0:T(8,128)(2,1)S(1)}, bf16[192,1152]{1,0:T(8,128)(2,1)S(1)}, u32[]{:S(2)}, u32[]{:S(2)}) collective-permute-start(bf16[192,1152]{1,0:T(8,128)(2,1)S(1)} %pad_maximum_fusion.3), channel_id=1, source_target_pairs={{0,1},{1,0},{2,3},{3,2},{4,5},{5,4},{6,7},{7,6},{8,9},{9,8},{10,11... | collective-permute-start | bytes 1327112 | tf_op jit(solution)/shard_map/ppermute | solution.py:24
  58.0 0.4 select_dynamic-update-slice_fusion
  58.3 0.9 collective-permute-done.7
  59.4 4.1 %fusion.4 = bf16[1024,1024]{1,0:T(8,128)(2,1)S(1)} fusion(bf16[1024,1152]{1,0:T(8,128)(2,1)S(1)} %fusion.21, bf16[1024,1152]{1,0:T(8,128)(2,1)S(1)} %select_dynamic-update-slice_fusion, f32[]{:T(128)} %bitcast.15, f32[]{:T(128)} %bitcast.5, s32[1024]{0:T(1024)S(1)} %bitcast.20, s32[1024]{0:T(1024)S(1)} %bitcast.21), kind=kOutput, calls=%fused_computation.6 | convolution fusion | flops 2427453440 | bytes 6823944 | tf_op jit(solution)/shard_map/dot_general | solution.py:82
  63.5 2.9 %fusion.27 = (bf16[1024,1152]{1,0:T(8,128)(2,1)S(1)}, f32[1024,1152]{1,0:T(8,128)S(1)}) fusion(bf16[1024,1024]{1,0:T(8,128)(2,1)S(1)} %fusion.4, bf16[1024,1152]{1,0:T(8,128)(2,1)S(1)} %select_dynamic-update-slice_fusion), kind=kOutput, calls=%fused_computation.70 | convolution fusion | flops 2417098752 | bytes 11534336 | tf_op jit(solution)/shard_map/dot_general | solution.py:234
  66.6 0.5 collective-permute-start.16
  67.0 3.0 %fusion.26 = (bf16[1024,1152]{1,0:T(8,128)(2,1)S(1)}, f32[1024,1152]{1,0:T(8,128)S(1)}) fusion(bf16[1024,1024]{1,0:T(8,128)(2,1)S(1)} %fusion.4, bf16[1024,1152]{1,0:T(8,128)(2,1)S(1)} %fusion.21), kind=kOutput, calls=%fused_computation.69 | convolution fusion | flops 2417098752 | bytes 11534336 | tf_op jit(solution)/shard_map/dot_general | solution.py:231
  70.0 0.2 slice.142
  70.2 0.1 slice.195
  70.4 4.1 %collective-permute-start.24 = (bf16[128,1152]{1,0:T(8,128)(2,1)S(1)}, bf16[128,1152]{1,0:T(8,128)(2,1)S(1)}, u32[]{:S(2)}, u32[]{:S(2)}) collective-permute-start(bf16[128,1152]{1,0:T(8,128)(2,1)S(1)} %get-tuple-element.18), channel_id=1, source_target_pairs={{0,8},{1,9},{2,10},{3,11},{4,12},{5,13},{6,14},{7,15},{8,0},{9,1},... | collective-permute-start | bytes 884744 | tf_op jit(solution)/shard_map/ppermute | solution.py:24
  74.5 1.6 %collective-permute-start.23 = (bf16[128,1152]{1,0:T(8,128)(2,1)S(1)}, bf16[128,1152]{1,0:T(8,128)(2,1)S(1)}, u32[]{:S(2)}, u32[]{:S(2)}) collective-permute-start(bf16[128,1152]{1,0:T(8,128)(2,1)S(1)} %get-tuple-element.19), channel_id=1, source_target_pairs={{0,4},{1,5},{2,6},{3,7},{4,8},{5,9},{6,10},{7,11},{8,12},{9,13},{1... | collective-permute-start | bytes 884744 | tf_op jit(solution)/shard_map/ppermute | solution.py:24
  76.1 1.7 %collective-permute-start.22 = (bf16[128,1152]{1,0:T(8,128)(2,1)S(1)}, bf16[128,1152]{1,0:T(8,128)(2,1)S(1)}, u32[]{:S(2)}, u32[]{:S(2)}) collective-permute-start(bf16[128,1152]{1,0:T(8,128)(2,1)S(1)} %get-tuple-element.17), channel_id=1, source_target_pairs={{0,12},{1,13},{2,14},{3,15},{4,0},{5,1},{6,2},{7,3},{8,4},{9,5},{1... | collective-permute-start | bytes 884744 | tf_op jit(solution)/shard_map/ppermute | solution.py:24
  77.8 1.3 collective-permute-start.26
  79.1 0.1 fusion.17
  79.2 2.5 %collective-permute-start.18 = (bf16[128,1152]{1,0:T(8,128)(2,1)S(1)}, bf16[128,1152]{1,0:T(8,128)(2,1)S(1)}, u32[]{:S(2)}, u32[]{:S(2)}) collective-permute-start(bf16[128,1152]{1,0:T(8,128)(2,1)S(1)} %get-tuple-element.16), channel_id=1, source_target_pairs={{0,112},{1,17},{2,114},{3,19},{4,116},{5,21},{6,118},{7,23},{8,120... | collective-permute-start | bytes 884744 | tf_op jit(solution)/shard_map/ppermute | solution.py:24
  81.7 0.1 collective-permute-done.24
  81.8 2.7 %collective-permute-start.19 = (bf16[64,1152]{1,0:T(8,128)(2,1)S(1)}, bf16[64,1152]{1,0:T(8,128)(2,1)S(1)}, u32[]{:S(2)}, u32[]{:S(2)}) collective-permute-start(bf16[64,1152]{1,0:T(8,128)(2,1)S(1)} %add_convert_fusion), channel_id=1, source_target_pairs={{0,96},{1,33},{2,98},{3,35},{4,100},{5,37},{6,102},{7,39},{8,104},... | collective-permute-start | bytes 442376 | tf_op jit(solution)/shard_map/ppermute | solution.py:24
  84.5 6.6 %collective-permute-done.23 = bf16[128,1152]{1,0:T(8,128)(2,1)S(1)} collective-permute-done((bf16[128,1152]{1,0:T(8,128)(2,1)S(1)}, bf16[128,1152]{1,0:T(8,128)(2,1)S(1)}, u32[]{:S(2)}, u32[]{:S(2)}) %collective-permute-start.23) | collective-permute-done | bytes 294944 | tf_op jit(solution)/shard_map/ppermute | solution.py:24
  91.1 0.1 fusion.12
  91.3 4.9 %collective-permute-start.30 = (bf16[128,1152]{1,0:T(8,128)(2,1)S(1)}, bf16[128,1152]{1,0:T(8,128)(2,1)S(1)}, u32[]{:S(2)}, u32[]{:S(2)}) collective-permute-start(bf16[128,1152]{1,0:T(8,128)(2,1)S(1)} %fusion.12), channel_id=1, source_target_pairs={{128,130},{129,131},{130,128},{131,129},{132,134},{133,135},{134,1... | collective-permute-start | bytes 884744 | tf_op jit(solution)/shard_map/ppermute | solution.py:24
  96.2 2.4 %collective-permute-start.17 = (bf16[128,1152]{1,0:T(8,128)(2,1)S(1)}, bf16[128,1152]{1,0:T(8,128)(2,1)S(1)}, u32[]{:S(2)}, u32[]{:S(2)}) collective-permute-start(bf16[128,1152]{1,0:T(8,128)(2,1)S(1)} %get-tuple-element.15), channel_id=1, source_target_pairs={{0,112},{1,17},{2,114},{3,19},{4,116},{5,21},{6,118},{7,23},{8,120... | collective-permute-start | bytes 884744 | tf_op jit(solution)/shard_map/ppermute | solution.py:24
  98.6 0.2 fusion.16
  98.7 0.1 collective-permute-start.20
  98.8 0.3 fusion.23
  99.1 5.5 %collective-permute-done.17 = bf16[128,1152]{1,0:T(8,128)(2,1)S(1)} collective-permute-done((bf16[128,1152]{1,0:T(8,128)(2,1)S(1)}, bf16[128,1152]{1,0:T(8,128)(2,1)S(1)}, u32[]{:S(2)}, u32[]{:S(2)}) %collective-permute-start.17) | collective-permute-done | bytes 294944 | tf_op jit(solution)/shard_map/ppermute | solution.py:24
  104.6 3.9 %collective-permute-done.20 = bf16[128,1152]{1,0:T(8,128)(2,1)S(1)} collective-permute-done((bf16[128,1152]{1,0:T(8,128)(2,1)S(1)}, bf16[128,1152]{1,0:T(8,128)(2,1)S(1)}, u32[]{:S(2)}, u32[]{:S(2)}) %collective-permute-start.20) | collective-permute-done | bytes 294944 | tf_op jit(solution)/shard_map/ppermute | solution.py:24
  108.5 0.1 fusion.22
  108.6 4.1 %collective-permute-start.21 = (bf16[128,1152]{1,0:T(8,128)(2,1)S(1)}, bf16[128,1152]{1,0:T(8,128)(2,1)S(1)}, u32[]{:S(2)}, u32[]{:S(2)}) collective-permute-start(bf16[128,1152]{1,0:T(8,128)(2,1)S(1)} %fusion.22), channel_id=1, source_target_pairs={{0,1},{1,0},{2,3},{3,2},{4,5},{5,4},{6,7},{7,6},{8,9},{9,8},{10,11... | collective-permute-start | bytes 884744 | tf_op jit(solution)/shard_map/ppermute | solution.py:24
  112.8 0.1 collective-permute-start.29
  112.9 1.1 collective-permute-start.28
  114.1 0.4 collective-permute-start.27
  114.5 0.2 fusion.20
  114.7 1.9 %collective-permute-start.25 = (bf16[128,1152]{1,0:T(8,128)(2,1)S(1)}, bf16[128,1152]{1,0:T(8,128)(2,1)S(1)}, u32[]{:S(2)}, u32[]{:S(2)}) collective-permute-start(bf16[128,1152]{1,0:T(8,128)(2,1)S(1)} %fusion.20), channel_id=1, source_target_pairs={{0,130},{1,129},{2,128},{3,131},{4,134},{5,133},{6,132},{7,135},{8... | collective-permute-start | bytes 884744 | tf_op jit(solution)/shard_map/ppermute | solution.py:24
  116.6 6.4 %collective-permute-done.29 = bf16[128,1152]{1,0:T(8,128)(2,1)S(1)} collective-permute-done((bf16[128,1152]{1,0:T(8,128)(2,1)S(1)}, bf16[128,1152]{1,0:T(8,128)(2,1)S(1)}, u32[]{:S(2)}, u32[]{:S(2)}) %collective-permute-start.29) | collective-permute-done | bytes 294944 | tf_op jit(solution)/shard_map/ppermute | solution.py:24
  123.0 4.9 %collective-permute-done.28 = bf16[128,1152]{1,0:T(8,128)(2,1)S(1)} collective-permute-done((bf16[128,1152]{1,0:T(8,128)(2,1)S(1)}, bf16[128,1152]{1,0:T(8,128)(2,1)S(1)}, u32[]{:S(2)}, u32[]{:S(2)}) %collective-permute-start.28) | collective-permute-done | bytes 294944 | tf_op jit(solution)/shard_map/ppermute | solution.py:24
  127.9 1.8 %collective-permute-done.27 = bf16[128,1152]{1,0:T(8,128)(2,1)S(1)} collective-permute-done((bf16[128,1152]{1,0:T(8,128)(2,1)S(1)}, bf16[128,1152]{1,0:T(8,128)(2,1)S(1)}, u32[]{:S(2)}, u32[]{:S(2)}) %collective-permute-start.27) | collective-permute-done | bytes 294944 | tf_op jit(solution)/shard_map/ppermute | solution.py:24
  129.7 1.2 fusion.6
  (55 shorter events, 1.3 us)
Async XLA Ops:
  0.0 9.2 %copy-start = (s32[16384]{0:T(1024)S(1)}, s32[16384]{0:T(1024)}, u32[]{:S(2)}) copy-start(s32[16384]{0:T(1024)} %param.12) | copy-start | bytes 196612
  0.0 9.1 %copy-start.2 = (s32[8]{0:T(128)S(1)}, s32[8]{0:T(128)}, u32[]{:S(2)}) copy-start(s32[8]{0:T(128)} %constant.39.clone) | copy-start | bytes 100
  0.0 9.1 %copy-start.3 = (s32[8]{0:T(128)S(1)}, s32[8]{0:T(128)}, u32[]{:S(2)}) copy-start(s32[8]{0:T(128)} %constant.38.clone) | copy-start | bytes 100
  0.0 9.3 %copy-start.4 = (s32[8]{0:T(128)S(1)}, s32[8]{0:T(128)}, u32[]{:S(2)}) copy-start(s32[8]{0:T(128)} %constant.37.clone) | copy-start | bytes 100
  3.4 7.7 %collective-permute-start = (bf16[128,1152]{1,0:T(8,128)(2,1)}, bf16[128,1152]{1,0:T(8,128)(2,1)S(1)}, u32[]{:S(2)}, u32[]{:S(2)}) collective-permute-start(bf16[128,1152]{1,0:T(8,128)(2,1)} %embed.1), channel_id=1, source_target_pairs={{1,129},{3,131},{5,133},{7,135},{9,137},{11,139},{13,141},{15,143}... | collective-permute-start | bytes 884744 | tf_op jit(solution)/shard_map/ppermute | solution.py:24
  5.6 8.5 %collective-permute-start.14 = (bf16[128,1152]{1,0:T(8,128)(2,1)}, bf16[128,1152]{1,0:T(8,128)(2,1)S(1)}, u32[]{:S(2)}, u32[]{:S(2)}) collective-permute-start(bf16[128,1152]{1,0:T(8,128)(2,1)} %embed.1), channel_id=1, source_target_pairs={{0,8},{1,9},{2,10},{3,11},{4,12},{5,13},{6,14},{7,15},{8,0},{9,1},... | collective-permute-start | bytes 884744 | tf_op jit(solution)/shard_map/ppermute | solution.py:24
  7.7 14.9 %collective-permute-start.13 = (bf16[128,1152]{1,0:T(8,128)(2,1)}, bf16[128,1152]{1,0:T(8,128)(2,1)S(1)}, u32[]{:S(2)}, u32[]{:S(2)}) collective-permute-start(bf16[128,1152]{1,0:T(8,128)(2,1)} %embed.1), channel_id=1, source_target_pairs={{0,12},{1,13},{2,14},{3,15},{4,0},{5,1},{6,2},{7,3},{8,4},{9,5},{1... | collective-permute-start | bytes 884744 | tf_op jit(solution)/shard_map/ppermute | solution.py:24
  8.7 13.9 %collective-permute-start.12 = (bf16[128,1152]{1,0:T(8,128)(2,1)}, bf16[128,1152]{1,0:T(8,128)(2,1)S(1)}, u32[]{:S(2)}, u32[]{:S(2)}) collective-permute-start(bf16[128,1152]{1,0:T(8,128)(2,1)} %embed.1), channel_id=1, source_target_pairs={{0,4},{1,5},{2,6},{3,7},{4,8},{5,9},{6,10},{7,11},{8,12},{9,13},{1... | collective-permute-start | bytes 884744 | tf_op jit(solution)/shard_map/ppermute | solution.py:24
  11.1 17.4 %collective-permute-start.1 = (bf16[128,1152]{1,0:T(8,128)(2,1)S(1)}, bf16[128,1152]{1,0:T(8,128)(2,1)S(1)}, u32[]{:S(2)}, u32[]{:S(2)}) collective-permute-start(bf16[128,1152]{1,0:T(8,128)(2,1)S(1)} %broadcast_select_fusion.2), channel_id=1, source_target_pairs={{0,1},{1,0},{2,3},{3,2},{4,5},{5,4},{6,7},{7,6},{8,9},{9,8},{10,11... | collective-permute-start | bytes 884744 | tf_op jit(solution)/shard_map/ppermute | solution.py:24
  23.7 34.3 %collective-permute-start.15 = (bf16[512,1152]{1,0:T(8,128)(2,1)S(1)}, bf16[512,1152]{1,0:T(8,128)(2,1)S(1)}, u32[]{:S(2)}, u32[]{:S(2)}) collective-permute-start(bf16[512,1152]{1,0:T(8,128)(2,1)S(1)} %pad_maximum_fusion), channel_id=1, source_target_pairs={{128,0},{129,3},{130,2},{131,1},{132,4},{133,7},{134,6},{135,5},{1... | collective-permute-start | bytes 3538952 | tf_op jit(solution)/shard_map/ppermute | solution.py:24
  27.2 7.8 %collective-permute-start.8 = (bf16[128,1152]{1,0:T(8,128)(2,1)S(1)}, bf16[128,1152]{1,0:T(8,128)(2,1)S(1)}, u32[]{:S(2)}, u32[]{:S(2)}) collective-permute-start(bf16[128,1152]{1,0:T(8,128)(2,1)S(1)} %collective-permute-done), channel_id=1, source_target_pairs={{0,128},{1,131},{2,130},{3,129},{4,132},{5,135},{6,134},{7,133},{8... | collective-permute-start | bytes 884744 | tf_op jit(solution)/shard_map/ppermute | solution.py:24
  28.6 8.1 %collective-permute-start.2 = (bf16[128,1152]{1,0:T(8,128)(2,1)S(1)}, bf16[128,1152]{1,0:T(8,128)(2,1)S(1)}, u32[]{:S(2)}, u32[]{:S(2)}) collective-permute-start(bf16[128,1152]{1,0:T(8,128)(2,1)S(1)} %broadcast_select_fusion), channel_id=1, source_target_pairs={{0,16},{1,113},{2,18},{3,115},{4,20},{5,117},{6,22},{7,119},{8,24}... | collective-permute-start | bytes 884744 | tf_op jit(solution)/shard_map/ppermute | solution.py:24
  28.7 11.8 %collective-permute-start.3 = (bf16[128,1152]{1,0:T(8,128)(2,1)S(1)}, bf16[128,1152]{1,0:T(8,128)(2,1)S(1)}, u32[]{:S(2)}, u32[]{:S(2)}) collective-permute-start(bf16[128,1152]{1,0:T(8,128)(2,1)S(1)} %broadcast_select_fusion), channel_id=1, source_target_pairs={{0,32},{1,97},{2,34},{3,99},{4,36},{5,101},{6,38},{7,103},{8,40},{... | collective-permute-start | bytes 884744 | tf_op jit(solution)/shard_map/ppermute | solution.py:24
  35.1 8.1 %collective-permute-start.9 = (bf16[128,1152]{1,0:T(8,128)(2,1)S(1)}, bf16[128,1152]{1,0:T(8,128)(2,1)S(1)}, u32[]{:S(2)}, u32[]{:S(2)}) collective-permute-start(bf16[128,1152]{1,0:T(8,128)(2,1)S(1)} %get-tuple-element.14), channel_id=1, source_target_pairs={{0,4},{1,5},{2,6},{3,7},{4,8},{5,9},{6,10},{7,11},{8,12},{9,13},{1... | collective-permute-start | bytes 884744 | tf_op jit(solution)/shard_map/ppermute | solution.py:24
  36.4 8.1 %collective-permute-start.10 = (bf16[128,1152]{1,0:T(8,128)(2,1)S(1)}, bf16[128,1152]{1,0:T(8,128)(2,1)S(1)}, u32[]{:S(2)}, u32[]{:S(2)}) collective-permute-start(bf16[128,1152]{1,0:T(8,128)(2,1)S(1)} %get-tuple-element.14), channel_id=1, source_target_pairs={{0,12},{1,13},{2,14},{3,15},{4,0},{5,1},{6,2},{7,3},{8,4},{9,5},{1... | collective-permute-start | bytes 884744 | tf_op jit(solution)/shard_map/ppermute | solution.py:24
  36.7 14.6 %collective-permute-start.11 = (bf16[128,1152]{1,0:T(8,128)(2,1)S(1)}, bf16[128,1152]{1,0:T(8,128)(2,1)S(1)}, u32[]{:S(2)}, u32[]{:S(2)}) collective-permute-start(bf16[128,1152]{1,0:T(8,128)(2,1)S(1)} %get-tuple-element.14), channel_id=1, source_target_pairs={{0,8},{1,9},{2,10},{3,11},{4,12},{5,13},{6,14},{7,15},{8,0},{9,1},... | collective-permute-start | bytes 884744 | tf_op jit(solution)/shard_map/ppermute | solution.py:24
  40.6 17.3 %collective-permute-start.4 = (bf16[256,1152]{1,0:T(8,128)(2,1)S(1)}, bf16[256,1152]{1,0:T(8,128)(2,1)S(1)}, u32[]{:S(2)}, u32[]{:S(2)}) collective-permute-start(bf16[256,1152]{1,0:T(8,128)(2,1)S(1)} %pad_maximum_fusion.2), channel_id=1, source_target_pairs={{0,1},{1,0},{2,3},{3,2},{4,5},{5,4},{6,7},{7,6},{8,9},{9,8},{10,11... | collective-permute-start | bytes 1769480 | tf_op jit(solution)/shard_map/ppermute | solution.py:24
  42.3 15.6 %copy-start.1 = (bf16[128,1152]{1,0:T(8,128)(2,1)S(1)}, bf16[128,1152]{1,0:T(8,128)(2,1)}, u32[]{:S(2)}) copy-start(bf16[128,1152]{1,0:T(8,128)(2,1)} %embed.1) | copy-start | bytes 884740
  43.2 8.1 %collective-permute-start.6 = (bf16[64,1152]{1,0:T(8,128)(2,1)S(1)}, bf16[64,1152]{1,0:T(8,128)(2,1)S(1)}, u32[]{:S(2)}, u32[]{:S(2)}) collective-permute-start(bf16[64,1152]{1,0:T(8,128)(2,1)S(1)} %slice_select_fusion), channel_id=1, source_target_pairs={{0,32},{1,97},{2,34},{3,99},{4,36},{5,101},{6,38},{7,103},{8,40},{... | collective-permute-start | bytes 442376 | tf_op jit(solution)/shard_map/ppermute | solution.py:24
  44.5 8.8 %collective-permute-start.5 = (bf16[128,1152]{1,0:T(8,128)(2,1)S(1)}, bf16[128,1152]{1,0:T(8,128)(2,1)S(1)}, u32[]{:S(2)}, u32[]{:S(2)}) collective-permute-start(bf16[128,1152]{1,0:T(8,128)(2,1)S(1)} %collective-permute-done.3), channel_id=1, source_target_pairs={{0,16},{1,113},{2,18},{3,115},{4,20},{5,117},{6,22},{7,119},{8,24}... | collective-permute-start | bytes 884744 | tf_op jit(solution)/shard_map/ppermute | solution.py:24
  53.3 5.9 %collective-permute-start.7 = (bf16[192,1152]{1,0:T(8,128)(2,1)S(1)}, bf16[192,1152]{1,0:T(8,128)(2,1)S(1)}, u32[]{:S(2)}, u32[]{:S(2)}) collective-permute-start(bf16[192,1152]{1,0:T(8,128)(2,1)S(1)} %pad_maximum_fusion.3), channel_id=1, source_target_pairs={{0,1},{1,0},{2,3},{3,2},{4,5},{5,4},{6,7},{7,6},{8,9},{9,8},{10,11... | collective-permute-start | bytes 1327112 | tf_op jit(solution)/shard_map/ppermute | solution.py:24
  66.6 12.5 %collective-permute-start.16 = (bf16[448,1152]{1,0:T(8,128)(2,1)S(1)}, bf16[448,1152]{1,0:T(8,128)(2,1)S(1)}, u32[]{:S(2)}, u32[]{:S(2)}) collective-permute-start(bf16[448,1152]{1,0:T(8,128)(2,1)S(1)} %pad_maximum_fusion.1), channel_id=1, source_target_pairs={{0,1},{1,0},{2,3},{3,2},{4,5},{5,4},{6,7},{7,6},{8,9},{9,8},{10,11... | collective-permute-start | bytes 3096584 | tf_op jit(solution)/shard_map/ppermute | solution.py:24
  70.4 11.4 %collective-permute-start.24 = (bf16[128,1152]{1,0:T(8,128)(2,1)S(1)}, bf16[128,1152]{1,0:T(8,128)(2,1)S(1)}, u32[]{:S(2)}, u32[]{:S(2)}) collective-permute-start(bf16[128,1152]{1,0:T(8,128)(2,1)S(1)} %get-tuple-element.18), channel_id=1, source_target_pairs={{0,8},{1,9},{2,10},{3,11},{4,12},{5,13},{6,14},{7,15},{8,0},{9,1},... | collective-permute-start | bytes 884744 | tf_op jit(solution)/shard_map/ppermute | solution.py:24
  74.5 16.6 %collective-permute-start.23 = (bf16[128,1152]{1,0:T(8,128)(2,1)S(1)}, bf16[128,1152]{1,0:T(8,128)(2,1)S(1)}, u32[]{:S(2)}, u32[]{:S(2)}) collective-permute-start(bf16[128,1152]{1,0:T(8,128)(2,1)S(1)} %get-tuple-element.19), channel_id=1, source_target_pairs={{0,4},{1,5},{2,6},{3,7},{4,8},{5,9},{6,10},{7,11},{8,12},{9,13},{1... | collective-permute-start | bytes 884744 | tf_op jit(solution)/shard_map/ppermute | solution.py:24
  76.1 15.0 %collective-permute-start.22 = (bf16[128,1152]{1,0:T(8,128)(2,1)S(1)}, bf16[128,1152]{1,0:T(8,128)(2,1)S(1)}, u32[]{:S(2)}, u32[]{:S(2)}) collective-permute-start(bf16[128,1152]{1,0:T(8,128)(2,1)S(1)} %get-tuple-element.17), channel_id=1, source_target_pairs={{0,12},{1,13},{2,14},{3,15},{4,0},{5,1},{6,2},{7,3},{8,4},{9,5},{1... | collective-permute-start | bytes 884744 | tf_op jit(solution)/shard_map/ppermute | solution.py:24
  77.8 21.0 %collective-permute-start.26 = (bf16[512,1152]{1,0:T(8,128)(2,1)S(1)}, bf16[512,1152]{1,0:T(8,128)(2,1)S(1)}, u32[]{:S(2)}, u32[]{:S(2)}) collective-permute-start(bf16[512,1152]{1,0:T(8,128)(2,1)S(1)} %slice.195), channel_id=1, source_target_pairs={{0,128},{1,131},{2,130},{3,129},{4,132},{5,135},{6,134},{7,133},{8... | collective-permute-start | bytes 3538952 | tf_op jit(solution)/shard_map/ppermute | solution.py:24
  79.2 19.3 %collective-permute-start.18 = (bf16[128,1152]{1,0:T(8,128)(2,1)S(1)}, bf16[128,1152]{1,0:T(8,128)(2,1)S(1)}, u32[]{:S(2)}, u32[]{:S(2)}) collective-permute-start(bf16[128,1152]{1,0:T(8,128)(2,1)S(1)} %get-tuple-element.16), channel_id=1, source_target_pairs={{0,112},{1,17},{2,114},{3,19},{4,116},{5,21},{6,118},{7,23},{8,120... | collective-permute-start | bytes 884744 | tf_op jit(solution)/shard_map/ppermute | solution.py:24
  81.8 16.7 %collective-permute-start.19 = (bf16[64,1152]{1,0:T(8,128)(2,1)S(1)}, bf16[64,1152]{1,0:T(8,128)(2,1)S(1)}, u32[]{:S(2)}, u32[]{:S(2)}) collective-permute-start(bf16[64,1152]{1,0:T(8,128)(2,1)S(1)} %add_convert_fusion), channel_id=1, source_target_pairs={{0,96},{1,33},{2,98},{3,35},{4,100},{5,37},{6,102},{7,39},{8,104},... | collective-permute-start | bytes 442376 | tf_op jit(solution)/shard_map/ppermute | solution.py:24
  91.3 25.3 %collective-permute-start.30 = (bf16[128,1152]{1,0:T(8,128)(2,1)S(1)}, bf16[128,1152]{1,0:T(8,128)(2,1)S(1)}, u32[]{:S(2)}, u32[]{:S(2)}) collective-permute-start(bf16[128,1152]{1,0:T(8,128)(2,1)S(1)} %fusion.12), channel_id=1, source_target_pairs={{128,130},{129,131},{130,128},{131,129},{132,134},{133,135},{134,1... | collective-permute-start | bytes 884744 | tf_op jit(solution)/shard_map/ppermute | solution.py:24
  96.2 8.5 %collective-permute-start.17 = (bf16[128,1152]{1,0:T(8,128)(2,1)S(1)}, bf16[128,1152]{1,0:T(8,128)(2,1)S(1)}, u32[]{:S(2)}, u32[]{:S(2)}) collective-permute-start(bf16[128,1152]{1,0:T(8,128)(2,1)S(1)} %get-tuple-element.15), channel_id=1, source_target_pairs={{0,112},{1,17},{2,114},{3,19},{4,116},{5,21},{6,118},{7,23},{8,120... | collective-permute-start | bytes 884744 | tf_op jit(solution)/shard_map/ppermute | solution.py:24
  98.7 9.8 %collective-permute-start.20 = (bf16[128,1152]{1,0:T(8,128)(2,1)S(1)}, bf16[128,1152]{1,0:T(8,128)(2,1)S(1)}, u32[]{:S(2)}, u32[]{:S(2)}) collective-permute-start(bf16[128,1152]{1,0:T(8,128)(2,1)S(1)} %fusion.16), channel_id=1, source_target_pairs={{0,96},{1,33},{2,98},{3,35},{4,100},{5,37},{6,102},{7,39},{8,104},... | collective-permute-start | bytes 884744 | tf_op jit(solution)/shard_map/ppermute | solution.py:24
  108.6 5.9 %collective-permute-start.21 = (bf16[128,1152]{1,0:T(8,128)(2,1)S(1)}, bf16[128,1152]{1,0:T(8,128)(2,1)S(1)}, u32[]{:S(2)}, u32[]{:S(2)}) collective-permute-start(bf16[128,1152]{1,0:T(8,128)(2,1)S(1)} %fusion.22), channel_id=1, source_target_pairs={{0,1},{1,0},{2,3},{3,2},{4,5},{5,4},{6,7},{7,6},{8,9},{9,8},{10,11... | collective-permute-start | bytes 884744 | tf_op jit(solution)/shard_map/ppermute | solution.py:24
  112.8 10.2 %collective-permute-start.29 = (bf16[128,1152]{1,0:T(8,128)(2,1)S(1)}, bf16[128,1152]{1,0:T(8,128)(2,1)S(1)}, u32[]{:S(2)}, u32[]{:S(2)}) collective-permute-start(bf16[128,1152]{1,0:T(8,128)(2,1)S(1)} %get-tuple-element.21), channel_id=1, source_target_pairs={{0,8},{1,9},{2,10},{3,11},{4,12},{5,13},{6,14},{7,15},{8,0},{9,1},... | collective-permute-start | bytes 884744 | tf_op jit(solution)/shard_map/ppermute | solution.py:24
  112.9 14.9 %collective-permute-start.28 = (bf16[128,1152]{1,0:T(8,128)(2,1)S(1)}, bf16[128,1152]{1,0:T(8,128)(2,1)S(1)}, u32[]{:S(2)}, u32[]{:S(2)}) collective-permute-start(bf16[128,1152]{1,0:T(8,128)(2,1)S(1)} %get-tuple-element.22), channel_id=1, source_target_pairs={{0,4},{1,5},{2,6},{3,7},{4,8},{5,9},{6,10},{7,11},{8,12},{9,13},{1... | collective-permute-start | bytes 884744 | tf_op jit(solution)/shard_map/ppermute | solution.py:24
  114.1 15.6 %collective-permute-start.27 = (bf16[128,1152]{1,0:T(8,128)(2,1)S(1)}, bf16[128,1152]{1,0:T(8,128)(2,1)S(1)}, u32[]{:S(2)}, u32[]{:S(2)}) collective-permute-start(bf16[128,1152]{1,0:T(8,128)(2,1)S(1)} %get-tuple-element.20), channel_id=1, source_target_pairs={{0,12},{1,13},{2,14},{3,15},{4,0},{5,1},{6,2},{7,3},{8,4},{9,5},{1... | collective-permute-start | bytes 884744 | tf_op jit(solution)/shard_map/ppermute | solution.py:24
  114.7 15.0 %collective-permute-start.25 = (bf16[128,1152]{1,0:T(8,128)(2,1)S(1)}, bf16[128,1152]{1,0:T(8,128)(2,1)S(1)}, u32[]{:S(2)}, u32[]{:S(2)}) collective-permute-start(bf16[128,1152]{1,0:T(8,128)(2,1)S(1)} %fusion.20), channel_id=1, source_target_pairs={{0,130},{1,129},{2,128},{3,131},{4,134},{5,133},{6,132},{7,135},{8... | collective-permute-start | bytes 884744 | tf_op jit(solution)/shard_map/ppermute | solution.py:24
